TPU v7x, 512 devices: a whole 4x8x8 slice. The times are simulated.
512 devices in a mesh: gx: 4 (over y_hi), gy: 16 (over z, y_lo), gz: 8 (over x, core).
Axes of the slice: x: 4, y: 8 (y_hi: 4, y_lo: 2; y = y_hi * 2 + y_lo), z: 8, core: 2. Of those that a mesh axis runs over, the one named last changes fastest.
Arguments:
- nodal_scalar_values: float32 [3, 32, 128, 16384], P(None, 'gx', 'gy', 'gz'), may hold values from -6 to 6
- geometry: float32 [6, 4, 16, 2048], P(None, 'gx', 'gy', 'gz'), may hold values from -1.2 to 4, as said below
Outputs:
- assembled: float32 [3, 32, 128, 16384], P(None, 'gx', 'gy', 'gz')
Inputs may be any that keep to these rules, and one draw needn't show every extreme that they name: `geometry`: G00, G11 and G22 are positive; each off-diagonal factor is at most 0.3 times the root of the product of its two diagonal factors in magnitude.
All inputs are finite; a program needn't handle non-finite values.
Results may differ from a plain program's by a relative error of at most 0.00007.
Values sent between devices are 32-bit elements; how exact they have to be, the bound alone decides.
No kernel may reach another device: no remote copies, remote signals or barrier semaphores. Data moves between devices by JAX's collectives and lax.ppermute only.
A program may use at most 64 MiB of HBM per device.

v0:
```python
import jax
import jax.numpy as jnp
import numpy as np
from jax import lax
from jax.experimental import pallas as pl
from jax.experimental.pallas import tpu as pltpu
from jax.sharding import PartitionSpec as P


interior_points = [
    -0.8717401485096066,
    -0.5917001814331423,
    -0.2092992179024789,
    0.2092992179024789,
    0.5917001814331423,
    0.8717401485096066,
]
LANES = 128
BLOCK = 256
F32 = jnp.float32
BF16 = jnp.bfloat16


def legendre_seven(point):
    previous = 1.0
    current = point
    for order in range(1, 7):
        following = ((2 * order + 1) * point * current - order * previous) / (order + 1)
        previous = current
        current = following
    return current


def gll_tables():
    degree = 7
    points = [-1.0] + interior_points + [1.0]
    values = [legendre_seven(point) for point in points]
    node_count = degree + 1
    weights = np.array([2.0 / (degree * (degree + 1) * value * value) for value in values])
    derivative = np.zeros((node_count, node_count))
    for row_index in range(node_count):
        for col_index in range(node_count):
            if row_index != col_index:
                derivative[row_index, col_index] = values[row_index] / (
                    values[col_index] * (points[row_index] - points[col_index])
                )
    derivative[0, 0] = -degree * (degree + 1) / 4.0
    derivative[node_count - 1, node_count - 1] = degree * (degree + 1) / 4.0
    return (derivative.astype(np.float32).astype(np.float64), weights)


def split_table(table):
    high = np.asarray(table, np.float32).astype(jnp.bfloat16)
    low = (np.asarray(table, np.float64) - high.astype(np.float64)).astype(jnp.bfloat16)
    return high, low


def tables():
    derivative, weights = gll_tables()
    eye = np.eye(8)

    high, low = split_table(np.concatenate([np.kron(derivative, eye), np.kron(eye, derivative)], 0))
    grad_y = np.concatenate([high, high, low], 1)
    back = (derivative * weights[:, None]).T
    high, low = split_table(np.concatenate([np.kron(back, np.diag(weights)), np.kron(np.diag(weights), back)], 1))
    back_y = np.concatenate([high, high, low], 1)
    many = np.eye(BLOCK // 8)
    grad_z = np.concatenate(split_table(np.kron(many, derivative.T)), 0)
    back_z = np.concatenate(split_table(np.kron(many, derivative)), 0)
    spread = np.kron(np.eye(LANES)[:, : BLOCK // 8], np.ones((1, 8))).astype(jnp.bfloat16)
    weight_z = np.tile(weights, BLOCK // 8)[None].astype(np.float32)
    plane = np.tile(np.kron(weights, weights)[:, None], (1, BLOCK)).astype(np.float32)
    return grad_y, back_y, grad_z, back_z, spread, weight_z, plane


def x_matrices():
    derivative, weights = gll_tables()
    scaled = (derivative * weights[:, None]).T / weights[:, None]
    return derivative, scaled


def split(values):
    high = values.astype(BF16)
    return high, (values - high.astype(F32)).astype(BF16)


def dot(left, right):
    return jnp.dot(left, right, preferred_element_type=F32)


def lane_iota():
    return lax.broadcasted_iota(jnp.int32, (8, LANES), 1)


def operator_block(field, factor, gy_ref, by_ref, gz_ref, bz_ref, plane):
    forward, backward = x_matrices()
    count = field.shape[0] // 64
    high, low = split(field)
    grad_z = dot(high, gz_ref[:BLOCK]) + dot(low, gz_ref[:BLOCK]) + dot(high, gz_ref[BLOCK:])
    g = [factor[k : k + 1] for k in range(6)]
    fluxes = []
    along_y = []
    for c in range(count):
        mine = slice(64 * c, 64 * c + 64)
        both = dot(gy_ref[...], jnp.concatenate([high[mine], low[mine], high[mine]], 0))
        gx, gy = both[:64], both[64:]
        gz = grad_z[mine]
        fx = g[0] * gx + g[3] * gy + g[4] * gz
        fy = g[3] * gx + g[1] * gy + g[5] * gz
        fz = g[4] * gx + g[5] * gy + g[2] * gz
        fluxes.append(fz)
        fh, fl = split(jnp.concatenate([fx, fy], 0))
        along_y.append(dot(by_ref[...], jnp.concatenate([fh, fl, fh], 0)))
    fh, fl = split(jnp.concatenate(fluxes, 0))
    back = dot(fh, bz_ref[:BLOCK]) + dot(fl, bz_ref[:BLOCK]) + dot(fh, bz_ref[BLOCK:])
    return [
        along_y[c] + plane * back[64 * c : 64 * c + 64] for c in range(count)
    ]


def spread_rows(rows, spread, weight):
    first = rows.astype(BF16)
    rest = rows - first.astype(F32)
    second = rest.astype(BF16)
    third = (rest - second.astype(F32)).astype(BF16)
    return (dot(first, spread) + dot(second, spread) + dot(third, spread)) * weight


def load_kernel(
    u_hbm, geo_hbm, gy_hbm, by_hbm, gz_hbm, bz_hbm, spread_hbm, wz_hbm, plane_hbm,
    u_ref, factor_ref, gy_ref, by_ref, gz_ref, bz_ref, plane_ref, za_ref, zb_ref,
    geo_ref, spread_ref, wz_ref, sems,
):
    components = u_ref.shape[0]
    length = u_ref.shape[3]
    blocks = length // BLOCK
    per_block = BLOCK // 8
    copies = []
    ends = (pl.ds(0, LANES), pl.ds(length - LANES, LANES))
    middle = pl.ds(LANES, length - 2 * LANES)
    pairs = [(geo_hbm, geo_ref), (spread_hbm, spread_ref), (wz_hbm, wz_ref)]
    pairs += [(u_hbm.at[:, :, :, where], u_ref.at[:, :, :, where]) for where in ends]
    pairs += [(gz_hbm, gz_ref), (gy_hbm, gy_ref), (by_hbm, by_ref), (bz_hbm, bz_ref)]
    pairs += [(plane_hbm, plane_ref)]
    pairs += [(u_hbm.at[c, :, :, middle], u_ref.at[c, :, :, middle]) for c in range(components)]
    for k, (source, target) in enumerate(pairs):
        copies.append(pltpu.make_async_copy(source, target, sems.at[k]))
        copies[-1].start()
    for copy in copies[:3]:
        copy.wait()
    geo = jnp.concatenate(
        [geo_ref[k, 0] for k in range(6)] + [jnp.zeros((2, length // 8), F32)], 0
    )
    rows = []
    for block in range(blocks):
        start = block * per_block
        tile = geo[:, start // LANES * LANES : start // LANES * LANES + LANES]
        shift = start % LANES
        rows.append(pltpu.roll(tile, LANES - shift, 1) if shift else tile)
    expanded = spread_rows(jnp.concatenate(rows, 0), spread_ref[...], wz_ref[...])
    factor_ref[...] = expanded
    for copy in copies[3:10]:
        copy.wait()
    factor = jnp.concatenate([expanded[:8, :LANES], expanded[8 * blocks - 8 :, LANES:]], 1)
    sides = []
    for c in range(components):
        sides.append(jnp.concatenate([u_ref[c, :, :, where].reshape(64, LANES) for where in ends], 1))
    totals = operator_block(
        jnp.concatenate(sides, 0), factor, gy_ref, by_ref, gz_ref, bz_ref, plane_ref[...]
    )
    even_z = lax.rem(lax.axis_index("gz"), 2) == 0
    lane = lane_iota()
    low_plane = jnp.zeros((8, LANES), F32)
    high_plane = jnp.zeros((8, LANES), F32)
    for c in range(components):
        for x in range(8):
            slot = 8 * c + x
            begin = totals[c][8 * x : 8 * x + 8, :LANES]
            end = totals[c][8 * x : 8 * x + 8, LANES:]
            begin = pltpu.roll(begin, slot, 1) if slot else begin
            end = pltpu.roll(end, slot + 1, 1)
            low_plane = jnp.where(lane == slot, begin, low_plane)
            high_plane = jnp.where(lane == slot, end, high_plane)
    za_ref[...] = jnp.where(even_z, high_plane, low_plane)
    zb_ref[...] = jnp.where(even_z, low_plane, high_plane)
    for copy in copies[10:]:
        copy.wait()


def stiffness_kernel(
    u_ref, factor_ref, gy_ref, by_ref, gz_ref, bz_ref, plane_ref, za_ref, zb_ref,
    out_ref, xa_ref, xb_ref, ia_ref, ea_ref, yb_ref,
):
    components = u_ref.shape[0]
    length = u_ref.shape[3]
    blocks = length // BLOCK
    tiles = length // LANES

    def body(block, carry):
        where = pl.ds(pl.multiple_of(block * BLOCK, BLOCK), BLOCK)
        field = jnp.concatenate(
            [u_ref[c, :, :, where].reshape(64, BLOCK) for c in range(components)], 0
        )
        factor = factor_ref[pl.ds(pl.multiple_of(block * 8, 8), 8), :]
        totals = operator_block(field, factor, gy_ref, by_ref, gz_ref, bz_ref, plane_ref[...])
        for c in range(components):
            out_ref[c, :, :, where] = totals[c].reshape(8, 8, BLOCK)
        return carry

    lax.fori_loop(0, blocks, body, 0, unroll=8)

    even_x, even_y, even_z = parities()
    low, high = ordered(even_z, za_ref[...], zb_ref[...])
    position = lax.broadcasted_iota(jnp.int32, (8, length), 1)
    last = (position % 8 == 7) & (position != length - 1)
    initial = (position % 8 == 0) & (position != 0)
    for c in range(components):
        for x in range(8):
            row = out_ref[c, x]
            after = pltpu.roll(row, length - 1, 1)
            before = pltpu.roll(row, 1, 1)
            row = row + jnp.where(last, after, 0.0) + jnp.where(initial, before, 0.0)
            slot = 8 * c + x
            out_ref[c, x] = row
            out_ref[c, x, :, :LANES] = row[:, :LANES] + at_lane(low, slot, 0)
            out_ref[c, x, :, length - LANES :] = row[:, length - LANES :] + at_lane(
                high, slot, LANES - 1
            )

    for c in range(components):
        for t in range(tiles):
            where = slice(t * LANES, t * LANES + LANES)
            spot = c * tiles + t
            first_plane = out_ref[c, 0, :, where]
            last_plane = out_ref[c, 7, :, where]
            xa_ref[spot] = jnp.where(even_x, last_plane, first_plane)
            xb_ref[spot] = jnp.where(even_x, first_plane, last_plane)
            for x in range(8):
                first_row = out_ref[c, x, 0:1, where]
                last_row = out_ref[c, x, 7:8, where]
                row_a = jnp.where(even_y, last_row, first_row)
                yb_ref[spot, x : x + 1] = jnp.where(even_y, first_row, last_row)
                if x in (0, 7):
                    at = 6 * t + 2 * c + x // 7
                    ea_ref[at : at + 1] = row_a
                else:
                    at = 18 * t + 6 * c + x - 1
                    ia_ref[at : at + 1] = row_a


def ordered(even, first, second):
    return jnp.where(even, second, first), jnp.where(even, first, second)


def parities():
    x, y, z = [lax.axis_index(axis) for axis in ("gx", "gy", "gz")]
    return [lax.rem(index, 2) == 0 for index in (x + z, y + z, z)]


def at_lane(packed, slot, lane_to):
    shift = (lane_to - slot) % LANES
    moved = pltpu.roll(packed, shift, 1) if shift else packed
    return jnp.where(lane_iota() == lane_to, moved, 0.0)


def copy_kernel(in_ref, out_ref):
    out_ref[...] = in_ref[...]


def edge_kernel(ea_ref, yb_ref, xa_ref, xb_ref, outa_ref, outb_ref):
    tiles = ea_ref.shape[0] // 6
    components = xa_ref.shape[0] // tiles
    even_x, even_y, _ = parities()
    for c in range(components):
        for t in range(tiles):
            spot = c * tiles + t
            sides = ordered(even_x, xa_ref[spot], xb_ref[spot])
            outb_ref[spot] = yb_ref[spot]
            for k in range(2):
                at = 6 * t + 2 * c + k
                at = slice(at, at + 1)
                first, last = sides[k][0:1], sides[k][7:8]
                outa_ref[at] = ea_ref[at] + jnp.where(even_y, last, first)
                x = slice(7 * k, 7 * k + 1)
                outb_ref[spot, x] = yb_ref[spot, x] + jnp.where(even_y, first, last)


def final_kernel(
    local_ref, xa_ref, xb_ref, ia_ref, ea_ref, yb_ref, out_hbm, out_ref, sems
):
    components = local_ref.shape[0]
    tiles = local_ref.shape[3] // LANES
    even_x, even_y, _ = parities()
    sublane = lax.broadcasted_iota(jnp.int32, (8, LANES), 0)
    row_a = jnp.where(even_y, 7, 0)
    row_b = 7 - row_a
    is_a, is_b = sublane == row_a, sublane == row_b
    copies = []
    for c in range(components):
        for t in range(tiles):
            where = slice(t * LANES, t * LANES + LANES)
            spot = c * tiles + t
            below, above = ordered(even_x, xa_ref[spot], xb_ref[spot])
            for x in range(8):
                value = local_ref[c, x, :, where]
                if x in (0, 7):
                    value = value + (above if x else below)
                    at = 6 * t + 2 * c + x // 7
                    line = ea_ref[at : at + 1]
                else:
                    at = 18 * t + 6 * c + x - 1
                    line = ia_ref[at : at + 1]
                other = yb_ref[spot, x : x + 1]
                line = jnp.broadcast_to(line, (8, LANES))
                other = jnp.broadcast_to(other, (8, LANES))
                change = jnp.where(is_a, line, jnp.where(is_b, other, 0.0))
                out_ref[c, x, :, where] = value + change
        copies.append(pltpu.make_async_copy(out_ref.at[c], out_hbm.at[c], sems.at[c]))
        copies[-1].start()
    for copy in copies:
        copy.wait()


def pairs_from(start, count):
    found = []
    for i in range(start, count - 1, 2):
        found += [(i, i + 1), (i + 1, i)]
    return found


def exchange(array, axis, start):
    return lax.ppermute(array, axis, pairs_from(start, lax.axis_size(axis)))


def mixed_exchange(array, axis, side):
    depth = lax.axis_size("gz")
    found = []
    for z in range(depth):
        for i, j in pairs_from((side + z) % 2, lax.axis_size(axis)):
            found.append((i * depth + z, j * depth + z))
    return lax.ppermute(array, (axis, "gz"), found)


def call(kernel, outs, scratch=(), flops=1000000, **specs):
    shapes = [out if hasattr(out, "dtype") else jax.ShapeDtypeStruct(out, F32) for out in outs]
    return pl.pallas_call(
        kernel,
        out_shape=shapes,
        scratch_shapes=list(scratch),
        compiler_params=pltpu.CompilerParams(vmem_limit_bytes=24 * 1024 * 1024),
        cost_estimate=pl.CostEstimate(flops=flops, bytes_accessed=1000000, transcendentals=0),
        **specs,
    )


def local(nodal, geometry):
    components, _, _, length = nodal.shape
    tiles = length // LANES
    blocks = length // BLOCK
    face = (components * tiles, 8, LANES)
    inner = (components * tiles * 6, LANES)
    edge = (components * tiles * 2, LANES)
    tile = (8, LANES)
    constants = [jnp.asarray(table) for table in tables()]
    operands = [
        pltpu.with_memory_space_constraint(operand, pltpu.HBM)
        for operand in [nodal, geometry] + constants
    ]
    hbm = pl.BlockSpec(memory_space=pltpu.HBM)
    kept = [jax.ShapeDtypeStruct(constants[k].shape, constants[k].dtype) for k in (0, 1, 2, 3, 6)]
    loaded = call(
        load_kernel,
        [nodal.shape, (8 * blocks, BLOCK)] + kept + [tile, tile],
        [pltpu.VMEM(operands[k].shape, operands[k].dtype) for k in (1, 6, 7)]
        + [pltpu.SemaphoreType.DMA((10 + components,))],
        in_specs=[hbm] * len(operands),
    )(*operands)
    za = exchange(loaded[-2], "gz", 0)
    zb = exchange(loaded[-1], "gz", 1)
    result, xa, xb, ia, ea, yb = call(
        stiffness_kernel, [nodal.shape, face, face, inner, edge, face]
    )(*loaded[:-2], za, zb)
    xa = mixed_exchange(xa, "gx", 0)
    xb = mixed_exchange(xb, "gx", 1)
    ia = mixed_exchange(ia, "gy", 0)
    (ea,) = call(copy_kernel, [edge])(ea)
    ea, yb = call(edge_kernel, [edge, face])(ea, yb, xa, xb)
    yb = mixed_exchange(yb, "gy", 1)
    ea = mixed_exchange(ea, "gy", 0)
    (result,) = call(
        final_kernel,
        [nodal.shape],
        [pltpu.VMEM(nodal.shape, F32), pltpu.SemaphoreType.DMA((components,))],
        out_specs=[hbm],
    )(result, xa, xb, ia, ea, yb)
    return result


def solution(mesh):
    return jax.shard_map(
        local,
        mesh=mesh,
        in_specs=(P(None, "gx", "gy", "gz"), P(None, "gx", "gy", "gz")),
        out_specs=P(None, "gx", "gy", "gz"),
        check_vma=False,
    )
```

profile of v0, /device:TPU:230, one launch (start us, length us, event | category | flops | bytes accessed | tf_op | source)
XLA Modules:
  0.0 46.0 jit_solution(7124283408530491573)
XLA Ops:
  0.0 2.0 %shard_map.91 = (f32[3,8,8,2048]{3,2,1,0:T(8,128)S(1)}, f32[64,256]{1,0:T(8,128)S(1)}, bf16[128,192]{1,0:T(8,128)(2,1)S(1)}, bf16[64,384]{1,0:T(8,128)(2,1)S(1)}...) custom-call(f32[3,8,8,2048]{3,2,1,0:T(8,128)} %u_hbm.1, ...), custom_call_target="tpu_custom_call" | custom-call | flops 1000000 | bytes 1000000 | tf_op jit(solution)/shard_map/pallas_call | solution.py:371
  2.0 1.9 %collective-permute-start = (f32[8,128]{1,0:T(8,128)S(1)}, f32[8,128]{1,0:T(8,128)S(1)}, u32[]{:S(2)}, u32[]{:S(2)}) collective-permute-start(f32[8,128]{1,0:T(8,128)S(1)} %get-tuple-element.29), channel_id=1, source_target_pairs={{0,1},{1,0},{2,3},{3,2},{4,5},{5,4},{6,7},{7,6},{8,9},{9,8},{10,11... | collective-permute-start | bytes 12296 | tf_op jit(solution)/shard_map/ppermute | solution.py:332
  4.0 2.8 %collective-permute-start.1 = (f32[8,128]{1,0:T(8,128)S(1)}, f32[8,128]{1,0:T(8,128)S(1)}, u32[]{:S(2)}, u32[]{:S(2)}) collective-permute-start(f32[8,128]{1,0:T(8,128)S(1)} %get-tuple-element.30), channel_id=1, source_target_pairs={{1,2},{2,1},{3,4},{4,3},{5,6},{6,5},{9,10},{10,9},{11,12},{12,11},... | collective-permute-start | bytes 12296 | tf_op jit(solution)/shard_map/ppermute | solution.py:332
  6.8 0.0 collective-permute-done.za_ref
  6.8 2.1 %collective-permute-done.1.zb_ref = f32[8,128]{1,0:T(8,128)S(1)} collective-permute-done((f32[8,128]{1,0:T(8,128)S(1)}, f32[8,128]{1,0:T(8,128)S(1)}, u32[]{:S(2)}, u32[]{:S(2)}) %collective-permute-start.1) | collective-permute-done | bytes 4128 | tf_op jit(solution)/shard_map/ppermute | solution.py:332
  8.9 4.3 %shard_map.92 = (f32[3,8,8,2048]{3,2,1,0:T(8,128)S(1)}, f32[48,8,128]{2,1,0:T(8,128)S(1)}, f32[48,8,128]{2,1,0:T(8,128)S(1)}, f32[288,128]{1,0:T(8,128)S(1)}, f3...) custom-call(f32[3,8,8,2048]{3,2,1,0:T(8,128)S(1)} %get-tuple-element.22.u_ref, ...), custom_call_target="tpu_custom_call" | custom-call | flops 1000000 | bytes 1000000 | tf_op jit(solution)/shard_map/pallas_call | solution.py:380
  13.2 2.7 %collective-permute-start.2 = (f32[48,8,128]{2,1,0:T(8,128)S(1)}, f32[48,8,128]{2,1,0:T(8,128)S(1)}, u32[]{:S(2)}, u32[]{:S(2)}) collective-permute-start(f32[48,8,128]{2,1,0:T(8,128)S(1)} %get-tuple-element.32), channel_id=1, source_target_pairs={{0,128},{128,0},{256,384},{384,256},{129,257},{257,129},{2,130},{1... | collective-permute-start | bytes 589832 | tf_op jit(solution)/shard_map/ppermute | solution.py:341
  15.9 1.9 %collective-permute-start.3 = (f32[48,8,128]{2,1,0:T(8,128)S(1)}, f32[48,8,128]{2,1,0:T(8,128)S(1)}, u32[]{:S(2)}, u32[]{:S(2)}) collective-permute-start(f32[48,8,128]{2,1,0:T(8,128)S(1)} %get-tuple-element.33), channel_id=1, source_target_pairs={{128,256},{256,128},{1,129},{129,1},{257,385},{385,257},{130,258},... | collective-permute-start | bytes 589832 | tf_op jit(solution)/shard_map/ppermute | solution.py:341
  17.9 7.6 %collective-permute-done.2.xa_ref = f32[48,8,128]{2,1,0:T(8,128)S(1)} collective-permute-done((f32[48,8,128]{2,1,0:T(8,128)S(1)}, f32[48,8,128]{2,1,0:T(8,128)S(1)}, u32[]{:S(2)}, u32[]{:S(2)}) %collective-permute-start.2) | collective-permute-done | bytes 196640 | tf_op jit(solution)/shard_map/ppermute | solution.py:341
  25.5 4.2 %collective-permute-done.3.xb_ref = f32[48,8,128]{2,1,0:T(8,128)S(1)} collective-permute-done((f32[48,8,128]{2,1,0:T(8,128)S(1)}, f32[48,8,128]{2,1,0:T(8,128)S(1)}, u32[]{:S(2)}, u32[]{:S(2)}) %collective-permute-start.3) | collective-permute-done | bytes 196640 | tf_op jit(solution)/shard_map/ppermute | solution.py:341
  29.7 0.1 shard_map.94
  29.9 1.9 %collective-permute-start.6 = (f32[48,8,128]{2,1,0:T(8,128)S(1)}, f32[48,8,128]{2,1,0:T(8,128)S(1)}, u32[]{:S(2)}, u32[]{:S(2)}) collective-permute-start(f32[48,8,128]{2,1,0:T(8,128)S(1)} %get-tuple-element.38), channel_id=1, source_target_pairs={{8,16},{16,8},{24,32},{32,24},{40,48},{48,40},{56,64},{64,56},{72,... | collective-permute-start | bytes 589832 | tf_op jit(solution)/shard_map/ppermute | solution.py:341
  31.8 6.9 %collective-permute-start.4 = (f32[288,128]{1,0:T(8,128)S(1)}, f32[288,128]{1,0:T(8,128)S(1)}, u32[]{:S(2)}, u32[]{:S(2)}) collective-permute-start(f32[288,128]{1,0:T(8,128)S(1)} %get-tuple-element.34), channel_id=1, source_target_pairs={{0,8},{8,0},{16,24},{24,16},{32,40},{40,32},{48,56},{56,48},{64,72... | collective-permute-start | bytes 442376 | tf_op jit(solution)/shard_map/ppermute | solution.py:341
  38.7 1.9 %collective-permute-start.5 = (f32[96,128]{1,0:T(8,128)S(1)}, f32[96,128]{1,0:T(8,128)S(1)}, u32[]{:S(2)}, u32[]{:S(2)}) collective-permute-start(f32[96,128]{1,0:T(8,128)S(1)} %get-tuple-element.37), channel_id=1, source_target_pairs={{0,8},{8,0},{16,24},{24,16},{32,40},{40,32},{48,56},{56,48},{64,72... | collective-permute-start | bytes 147464 | tf_op jit(solution)/shard_map/ppermute | solution.py:341
  40.7 1.4 %collective-permute-done.4.ia_ref = f32[288,128]{1,0:T(8,128)S(1)} collective-permute-done((f32[288,128]{1,0:T(8,128)S(1)}, f32[288,128]{1,0:T(8,128)S(1)}, u32[]{:S(2)}, u32[]{:S(2)}) %collective-permute-start.4) | collective-permute-done | bytes 147488 | tf_op jit(solution)/shard_map/ppermute | solution.py:341
  42.0 2.7 %collective-permute-done.5.ea_ref = f32[96,128]{1,0:T(8,128)S(1)} collective-permute-done((f32[96,128]{1,0:T(8,128)S(1)}, f32[96,128]{1,0:T(8,128)S(1)}, u32[]{:S(2)}, u32[]{:S(2)}) %collective-permute-start.5) | collective-permute-done | bytes 49184 | tf_op jit(solution)/shard_map/ppermute | solution.py:341
  44.7 0.0 collective-permute-done.6.yb_ref
  44.7 1.3 %shard_map.95 = f32[3,8,8,2048]{3,2,1,0:T(8,128)} custom-call(f32[3,8,8,2048]{3,2,1,0:T(8,128)S(1)} %get-tuple-element.31.local_ref, f32[48,8,128]{2,1,0:T(8,128)S(1)} %collective-permute-done.2.xa_ref, f32[48,8,128]{2,1,0:T(8,128)S(1)} %collective-permute-done.3.xb_ref, f32[288,128]{1,0:T(8,128)S(1)} %collective-permute-done.4.ia_ref, ...), custom_call_target="tpu_custom_call" | custom-call | flops 1000000 | bytes 1000000 | tf_op jit(solution)/shard_map/pallas_call | solution.py:390
  (1 shorter events, 0.0 us)
Async XLA Ops:
  2.0 4.8 %collective-permute-start = (f32[8,128]{1,0:T(8,128)S(1)}, f32[8,128]{1,0:T(8,128)S(1)}, u32[]{:S(2)}, u32[]{:S(2)}) collective-permute-start(f32[8,128]{1,0:T(8,128)S(1)} %get-tuple-element.29), channel_id=1, source_target_pairs={{0,1},{1,0},{2,3},{3,2},{4,5},{5,4},{6,7},{7,6},{8,9},{9,8},{10,11... | collective-permute-start | bytes 12296 | tf_op jit(solution)/shard_map/ppermute | solution.py:332
  4.0 4.9 %collective-permute-start.1 = (f32[8,128]{1,0:T(8,128)S(1)}, f32[8,128]{1,0:T(8,128)S(1)}, u32[]{:S(2)}, u32[]{:S(2)}) collective-permute-start(f32[8,128]{1,0:T(8,128)S(1)} %get-tuple-element.30), channel_id=1, source_target_pairs={{1,2},{2,1},{3,4},{4,3},{5,6},{6,5},{9,10},{10,9},{11,12},{12,11},... | collective-permute-start | bytes 12296 | tf_op jit(solution)/shard_map/ppermute | solution.py:332
  13.2 12.3 %collective-permute-start.2 = (f32[48,8,128]{2,1,0:T(8,128)S(1)}, f32[48,8,128]{2,1,0:T(8,128)S(1)}, u32[]{:S(2)}, u32[]{:S(2)}) collective-permute-start(f32[48,8,128]{2,1,0:T(8,128)S(1)} %get-tuple-element.32), channel_id=1, source_target_pairs={{0,128},{128,0},{256,384},{384,256},{129,257},{257,129},{2,130},{1... | collective-permute-start | bytes 589832 | tf_op jit(solution)/shard_map/ppermute | solution.py:341
  15.9 13.8 %collective-permute-start.3 = (f32[48,8,128]{2,1,0:T(8,128)S(1)}, f32[48,8,128]{2,1,0:T(8,128)S(1)}, u32[]{:S(2)}, u32[]{:S(2)}) collective-permute-start(f32[48,8,128]{2,1,0:T(8,128)S(1)} %get-tuple-element.33), channel_id=1, source_target_pairs={{128,256},{256,128},{1,129},{129,1},{257,385},{385,257},{130,258},... | collective-permute-start | bytes 589832 | tf_op jit(solution)/shard_map/ppermute | solution.py:341
  29.9 14.9 %collective-permute-start.6 = (f32[48,8,128]{2,1,0:T(8,128)S(1)}, f32[48,8,128]{2,1,0:T(8,128)S(1)}, u32[]{:S(2)}, u32[]{:S(2)}) collective-permute-start(f32[48,8,128]{2,1,0:T(8,128)S(1)} %get-tuple-element.38), channel_id=1, source_target_pairs={{8,16},{16,8},{24,32},{32,24},{40,48},{48,40},{56,64},{64,56},{72,... | collective-permute-start | bytes 589832 | tf_op jit(solution)/shard_map/ppermute | solution.py:341
  31.8 10.2 %collective-permute-start.4 = (f32[288,128]{1,0:T(8,128)S(1)}, f32[288,128]{1,0:T(8,128)S(1)}, u32[]{:S(2)}, u32[]{:S(2)}) collective-permute-start(f32[288,128]{1,0:T(8,128)S(1)} %get-tuple-element.34), channel_id=1, source_target_pairs={{0,8},{8,0},{16,24},{24,16},{32,40},{40,32},{48,56},{56,48},{64,72... | collective-permute-start | bytes 442376 | tf_op jit(solution)/shard_map/ppermute | solution.py:341
  38.7 6.0 %collective-permute-start.5 = (f32[96,128]{1,0:T(8,128)S(1)}, f32[96,128]{1,0:T(8,128)S(1)}, u32[]{:S(2)}, u32[]{:S(2)}) collective-permute-start(f32[96,128]{1,0:T(8,128)S(1)} %get-tuple-element.37), channel_id=1, source_target_pairs={{0,8},{8,0},{16,24},{24,16},{32,40},{40,32},{48,56},{56,48},{64,72... | collective-permute-start | bytes 147464 | tf_op jit(solution)/shard_map/ppermute | solution.py:341
where the time goes:
time: 46.3 us; the launch traced here: 46 us
  starting transfers between devices  20.2 us (44%)
  waiting for transfers between devices  18 us (39%)
  Pallas kernels  7.79 us (17%)
    ppermute x5, waiting for transfers between devices, mixed_exchange(): return lax.ppermute(array, (axis, 'gz'), found)  15.9 us
    ppermute x5, starting transfers between devices, mixed_exchange(): return lax.ppermute(array, (axis, 'gz'), found)  15.4 us
    ppermute x2, starting transfers between devices, exchange(): return lax.ppermute(array, axis, pairs_from(start, lax.axis_size(axis)))  4.76 us
    pallas_call x1, Pallas kernels, local(): call(stiffness_kernel, [nodal.shape, face, face, inner, edge, face])  4.33 us
    ppermute x2, waiting for transfers between devices, exchange(): return lax.ppermute(array, axis, pairs_from(start, lax.axis_size(axis)))  2.07 us
    pallas_call x1, Pallas kernels, local(): call(load_kernel, [nodal.shape, (8 * blocks, BLOCK)] + kept + [tile, tile...  2.04 us
    pallas_call x1, Pallas kernels, local(): call(final_kernel, [nodal.shape], [pltpu.VMEM(nodal.shape, F32), pltpu.Se...  1.28 us
  transfers between devices with their start and end apart: 7, of which 5 were waited for; matrix products, arithmetic and copies ran while one was open for 0% of the time, Pallas kernels for 0%

commit v1 on v0

--- a/solution.py
+++ b/solution.py
@@ -188,13 +188,10 @@
 
 
 def stiffness_kernel(
-    u_ref, factor_ref, gy_ref, by_ref, gz_ref, bz_ref, plane_ref, za_ref, zb_ref,
-    out_ref, xa_ref, xb_ref, ia_ref, ea_ref, yb_ref,
+    u_ref, factor_ref, gy_ref, by_ref, gz_ref, bz_ref, plane_ref, out_ref
 ):
     components = u_ref.shape[0]
-    length = u_ref.shape[3]
-    blocks = length // BLOCK
-    tiles = length // LANES
+    blocks = u_ref.shape[3] // BLOCK
 
     def body(block, carry):
         where = pl.ds(pl.multiple_of(block * BLOCK, BLOCK), BLOCK)
@@ -209,6 +206,13 @@
 
     lax.fori_loop(0, blocks, body, 0, unroll=8)
 
+
+def face_kernel(
+    in_ref, za_ref, zb_ref, out_ref, xa_ref, xb_ref, ia_ref, ea_ref, yb_ref
+):
+    components = in_ref.shape[0]
+    length = in_ref.shape[3]
+    tiles = length // LANES
     even_x, even_y, even_z = parities()
     low, high = ordered(even_z, za_ref[...], zb_ref[...])
     position = lax.broadcasted_iota(jnp.int32, (8, length), 1)
@@ -216,7 +220,7 @@
     initial = (position % 8 == 0) & (position != 0)
     for c in range(components):
         for x in range(8):
-            row = out_ref[c, x]
+            row = in_ref[c, x]
             after = pltpu.roll(row, length - 1, 1)
             before = pltpu.roll(row, 1, 1)
             row = row + jnp.where(last, after, 0.0) + jnp.where(initial, before, 0.0)
@@ -254,7 +258,7 @@
 
 def parities():
     x, y, z = [lax.axis_index(axis) for axis in ("gx", "gy", "gz")]
-    return [lax.rem(index, 2) == 0 for index in (x + z, y + z, z)]
+    return [lax.rem(index, 2) == 0 for index in (x + y + z, y, z)]
 
 
 def at_lane(packed, slot, lane_to):
@@ -332,13 +336,14 @@
     return lax.ppermute(array, axis, pairs_from(start, lax.axis_size(axis)))
 
 
-def mixed_exchange(array, axis, side):
-    depth = lax.axis_size("gz")
+def mixed_exchange(array, side):
+    width, height, depth = [lax.axis_size(axis) for axis in ("gx", "gy", "gz")]
     found = []
-    for z in range(depth):
-        for i, j in pairs_from((side + z) % 2, lax.axis_size(axis)):
-            found.append((i * depth + z, j * depth + z))
-    return lax.ppermute(array, (axis, "gz"), found)
+    for y in range(height):
+        for z in range(depth):
+            for i, j in pairs_from((side + y + z) % 2, width):
+                found.append(((i * height + y) * depth + z, (j * height + y) * depth + z))
+    return lax.ppermute(array, ("gx", "gy", "gz"), found)
 
 
 def call(kernel, outs, scratch=(), flops=1000000, **specs):
@@ -377,16 +382,17 @@
     )(*operands)
     za = exchange(loaded[-2], "gz", 0)
     zb = exchange(loaded[-1], "gz", 1)
+    (result,) = call(stiffness_kernel, [nodal.shape])(*loaded[:-2])
     result, xa, xb, ia, ea, yb = call(
-        stiffness_kernel, [nodal.shape, face, face, inner, edge, face]
-    )(*loaded[:-2], za, zb)
-    xa = mixed_exchange(xa, "gx", 0)
-    xb = mixed_exchange(xb, "gx", 1)
-    ia = mixed_exchange(ia, "gy", 0)
+        face_kernel, [nodal.shape, face, face, inner, edge, face]
+    )(result, za, zb)
+    xa = mixed_exchange(xa, 0)
+    xb = mixed_exchange(xb, 1)
+    ia = exchange(ia, "gy", 0)
     (ea,) = call(copy_kernel, [edge])(ea)
     ea, yb = call(edge_kernel, [edge, face])(ea, yb, xa, xb)
-    yb = mixed_exchange(yb, "gy", 1)
-    ea = mixed_exchange(ea, "gy", 0)
+    yb = exchange(yb, "gy", 1)
+    ea = exchange(ea, "gy", 0)
     (result,) = call(
         final_kernel,
         [nodal.shape],

time: 46.3 us -> 43.9 us (0.948)
  the two profiles are of different devices: /device:TPU:230 before, /device:TPU:208 now
where the time goes in v1:
time: 43.9 us; the launch traced here: 43.6 us
  starting transfers between devices  21.8 us (50%)
  waiting for transfers between devices  13.6 us (31%)
  Pallas kernels  8.18 us (19%)
    ppermute x5, starting transfers between devices, exchange(): return lax.ppermute(array, axis, pairs_from(start, lax.axis_size(axis)))  13.4 us
    ppermute x2, waiting for transfers between devices, mixed_exchange(): return lax.ppermute(array, ('gx', 'gy', 'gz'), found)  8.57 us
    ppermute x2, starting transfers between devices, mixed_exchange(): return lax.ppermute(array, ('gx', 'gy', 'gz'), found)  8.4 us
    ppermute x5, waiting for transfers between devices, exchange(): return lax.ppermute(array, axis, pairs_from(start, lax.axis_size(axis)))  5 us
    pallas_call x1, Pallas kernels, local(): result, = call(stiffness_kernel, [nodal.shape])(*loaded[:-2])  3.6 us
    pallas_call x1, Pallas kernels, local(): call(load_kernel, [nodal.shape, (8 * blocks, BLOCK)] + kept + [tile, tile...  2.04 us
    pallas_call x1, Pallas kernels, local(): call(final_kernel, [nodal.shape], [pltpu.VMEM(nodal.shape, F32), pltpu.Se...  1.28 us
    pallas_call x1, Pallas kernels, local(): call(face_kernel, [nodal.shape, face, face, inner, edge, face])  1.13 us
  transfers between devices with their start and end apart: 7, of which 3 were waited for; matrix products, arithmetic and copies ran while one was open for 0% of the time, Pallas kernels for 8%

profile of v1, /device:TPU:208, one launch (start us, length us, event | category | flops | bytes accessed | tf_op | source)
XLA Modules:
  0.0 43.6 jit_solution(11441902438766823034)
XLA Ops:
  0.0 2.0 %shard_map.91 = (f32[3,8,8,2048]{3,2,1,0:T(8,128)S(1)}, f32[64,256]{1,0:T(8,128)S(1)}, bf16[128,192]{1,0:T(8,128)(2,1)S(1)}, bf16[64,384]{1,0:T(8,128)(2,1)S(1)}...) custom-call(f32[3,8,8,2048]{3,2,1,0:T(8,128)} %u_hbm.1, ...), custom_call_target="tpu_custom_call" | custom-call | flops 1000000 | bytes 1000000 | tf_op jit(solution)/shard_map/pallas_call | solution.py:376
  2.0 1.9 %collective-permute-start = (f32[8,128]{1,0:T(8,128)S(1)}, f32[8,128]{1,0:T(8,128)S(1)}, u32[]{:S(2)}, u32[]{:S(2)}) collective-permute-start(f32[8,128]{1,0:T(8,128)S(1)} %get-tuple-element.29), channel_id=1, source_target_pairs={{0,1},{1,0},{2,3},{3,2},{4,5},{5,4},{6,7},{7,6},{8,9},{9,8},{10,11... | collective-permute-start | bytes 12296 | tf_op jit(solution)/shard_map/ppermute | solution.py:336
  4.0 0.7 %collective-permute-start.1 = (f32[8,128]{1,0:T(8,128)S(1)}, f32[8,128]{1,0:T(8,128)S(1)}, u32[]{:S(2)}, u32[]{:S(2)}) collective-permute-start(f32[8,128]{1,0:T(8,128)S(1)} %get-tuple-element.30), channel_id=1, source_target_pairs={{1,2},{2,1},{3,4},{4,3},{5,6},{6,5},{9,10},{10,9},{11,12},{12,11},... | collective-permute-start | bytes 12296 | tf_op jit(solution)/shard_map/ppermute | solution.py:336
  4.6 3.6 %shard_map.92.in_ref = f32[3,8,8,2048]{3,2,1,0:T(8,128)S(1)} custom-call(f32[3,8,8,2048]{3,2,1,0:T(8,128)S(1)} %get-tuple-element.22.u_ref, f32[64,256]{1,0:T(8,128)S(1)} %get-tuple-element.23.factor_ref, bf16[128,192]{1,0:T(8,128)(2,1)S(1)} %get-tuple-element.24.gy_ref, bf16[64,384]{1,0:T(8,128)(2,1)S(1)} %get-tuple-element.25.by_ref, ...), custom_call_target="tpu_custom_call" | custom-call | flops 1000000 | bytes 1000000 | tf_op jit(solution)/shard_map/pallas_call | solution.py:385
  8.3 0.0 collective-permute-done.za_ref
  8.3 0.0 collective-permute-done.1.zb_ref
  8.3 1.1 %shard_map.93 = (f32[3,8,8,2048]{3,2,1,0:T(8,128)S(1)}, f32[48,8,128]{2,1,0:T(8,128)S(1)}, f32[48,8,128]{2,1,0:T(8,128)S(1)}, f32[288,128]{1,0:T(8,128)S(1)}, f3...) custom-call(f32[3,8,8,2048]{3,2,1,0:T(8,128)S(1)} %shard_map.92.in_ref, f32[8,128]{1,0:T(8,128)S(1)} %collective-permute-done.za_ref, ...), custom_call_target="tpu_custom_call" | custom-call | flops 1000000 | bytes 1000000 | tf_op jit(solution)/shard_map/pallas_call | solution.py:386
  9.4 2.2 %collective-permute-start.2 = (f32[48,8,128]{2,1,0:T(8,128)S(1)}, f32[48,8,128]{2,1,0:T(8,128)S(1)}, u32[]{:S(2)}, u32[]{:S(2)}) collective-permute-start(f32[48,8,128]{2,1,0:T(8,128)S(1)} %get-tuple-element.32), channel_id=1, source_target_pairs={{0,128},{128,0},{256,384},{384,256},{129,257},{257,129},{2,130},{1... | collective-permute-start | bytes 589832 | tf_op jit(solution)/shard_map/ppermute | solution.py:346
  11.7 6.2 %collective-permute-start.3 = (f32[48,8,128]{2,1,0:T(8,128)S(1)}, f32[48,8,128]{2,1,0:T(8,128)S(1)}, u32[]{:S(2)}, u32[]{:S(2)}) collective-permute-start(f32[48,8,128]{2,1,0:T(8,128)S(1)} %get-tuple-element.33), channel_id=1, source_target_pairs={{128,256},{256,128},{1,129},{129,1},{257,385},{385,257},{130,258},... | collective-permute-start | bytes 589832 | tf_op jit(solution)/shard_map/ppermute | solution.py:346
  17.8 0.0 collective-permute-done.2.xa_ref
  17.9 8.5 %collective-permute-done.3.xb_ref = f32[48,8,128]{2,1,0:T(8,128)S(1)} collective-permute-done((f32[48,8,128]{2,1,0:T(8,128)S(1)}, f32[48,8,128]{2,1,0:T(8,128)S(1)}, u32[]{:S(2)}, u32[]{:S(2)}) %collective-permute-start.3) | collective-permute-done | bytes 196640 | tf_op jit(solution)/shard_map/ppermute | solution.py:346
  26.4 0.1 shard_map.95
  26.5 1.9 %collective-permute-start.6 = (f32[48,8,128]{2,1,0:T(8,128)S(1)}, f32[48,8,128]{2,1,0:T(8,128)S(1)}, u32[]{:S(2)}, u32[]{:S(2)}) collective-permute-start(f32[48,8,128]{2,1,0:T(8,128)S(1)} %get-tuple-element.38), channel_id=1, source_target_pairs={{8,16},{16,8},{24,32},{32,24},{40,48},{48,40},{56,64},{64,56},{72,... | collective-permute-start | bytes 589832 | tf_op jit(solution)/shard_map/ppermute | solution.py:336
  28.5 6.9 %collective-permute-start.4 = (f32[288,128]{1,0:T(8,128)S(1)}, f32[288,128]{1,0:T(8,128)S(1)}, u32[]{:S(2)}, u32[]{:S(2)}) collective-permute-start(f32[288,128]{1,0:T(8,128)S(1)} %get-tuple-element.34), channel_id=1, source_target_pairs={{0,8},{8,0},{16,24},{24,16},{32,40},{40,32},{48,56},{56,48},{64,72... | collective-permute-start | bytes 442376 | tf_op jit(solution)/shard_map/ppermute | solution.py:336
  35.4 1.9 %collective-permute-start.5 = (f32[96,128]{1,0:T(8,128)S(1)}, f32[96,128]{1,0:T(8,128)S(1)}, u32[]{:S(2)}, u32[]{:S(2)}) collective-permute-start(f32[96,128]{1,0:T(8,128)S(1)} %get-tuple-element.37), channel_id=1, source_target_pairs={{0,8},{8,0},{16,24},{24,16},{32,40},{40,32},{48,56},{56,48},{64,72... | collective-permute-start | bytes 147464 | tf_op jit(solution)/shard_map/ppermute | solution.py:336
  37.3 4.5 %collective-permute-done.4.ia_ref = f32[288,128]{1,0:T(8,128)S(1)} collective-permute-done((f32[288,128]{1,0:T(8,128)S(1)}, f32[288,128]{1,0:T(8,128)S(1)}, u32[]{:S(2)}, u32[]{:S(2)}) %collective-permute-start.4) | collective-permute-done | bytes 147488 | tf_op jit(solution)/shard_map/ppermute | solution.py:336
  41.8 0.5 %collective-permute-done.5.ea_ref = f32[96,128]{1,0:T(8,128)S(1)} collective-permute-done((f32[96,128]{1,0:T(8,128)S(1)}, f32[96,128]{1,0:T(8,128)S(1)}, u32[]{:S(2)}, u32[]{:S(2)}) %collective-permute-start.5) | collective-permute-done | bytes 49184 | tf_op jit(solution)/shard_map/ppermute | solution.py:336
  42.3 0.0 collective-permute-done.6.yb_ref
  42.3 1.3 %shard_map.96 = f32[3,8,8,2048]{3,2,1,0:T(8,128)} custom-call(f32[3,8,8,2048]{3,2,1,0:T(8,128)S(1)} %get-tuple-element.31.local_ref, f32[48,8,128]{2,1,0:T(8,128)S(1)} %collective-permute-done.2.xa_ref, f32[48,8,128]{2,1,0:T(8,128)S(1)} %collective-permute-done.3.xb_ref, f32[288,128]{1,0:T(8,128)S(1)} %collective-permute-done.4.ia_ref, ...), custom_call_target="tpu_custom_call" | custom-call | flops 1000000 | bytes 1000000 | tf_op jit(solution)/shard_map/pallas_call | solution.py:396
  (1 shorter events, 0.0 us)
Async XLA Ops:
  2.0 6.2 %collective-permute-start = (f32[8,128]{1,0:T(8,128)S(1)}, f32[8,128]{1,0:T(8,128)S(1)}, u32[]{:S(2)}, u32[]{:S(2)}) collective-permute-start(f32[8,128]{1,0:T(8,128)S(1)} %get-tuple-element.29), channel_id=1, source_target_pairs={{0,1},{1,0},{2,3},{3,2},{4,5},{5,4},{6,7},{7,6},{8,9},{9,8},{10,11... | collective-permute-start | bytes 12296 | tf_op jit(solution)/shard_map/ppermute | solution.py:336
  4.0 4.3 %collective-permute-start.1 = (f32[8,128]{1,0:T(8,128)S(1)}, f32[8,128]{1,0:T(8,128)S(1)}, u32[]{:S(2)}, u32[]{:S(2)}) collective-permute-start(f32[8,128]{1,0:T(8,128)S(1)} %get-tuple-element.30), channel_id=1, source_target_pairs={{1,2},{2,1},{3,4},{4,3},{5,6},{6,5},{9,10},{10,9},{11,12},{12,11},... | collective-permute-start | bytes 12296 | tf_op jit(solution)/shard_map/ppermute | solution.py:336
  9.4 8.5 %collective-permute-start.2 = (f32[48,8,128]{2,1,0:T(8,128)S(1)}, f32[48,8,128]{2,1,0:T(8,128)S(1)}, u32[]{:S(2)}, u32[]{:S(2)}) collective-permute-start(f32[48,8,128]{2,1,0:T(8,128)S(1)} %get-tuple-element.32), channel_id=1, source_target_pairs={{0,128},{128,0},{256,384},{384,256},{129,257},{257,129},{2,130},{1... | collective-permute-start | bytes 589832 | tf_op jit(solution)/shard_map/ppermute | solution.py:346
  11.7 14.7 %collective-permute-start.3 = (f32[48,8,128]{2,1,0:T(8,128)S(1)}, f32[48,8,128]{2,1,0:T(8,128)S(1)}, u32[]{:S(2)}, u32[]{:S(2)}) collective-permute-start(f32[48,8,128]{2,1,0:T(8,128)S(1)} %get-tuple-element.33), channel_id=1, source_target_pairs={{128,256},{256,128},{1,129},{129,1},{257,385},{385,257},{130,258},... | collective-permute-start | bytes 589832 | tf_op jit(solution)/shard_map/ppermute | solution.py:346
  26.5 15.8 %collective-permute-start.6 = (f32[48,8,128]{2,1,0:T(8,128)S(1)}, f32[48,8,128]{2,1,0:T(8,128)S(1)}, u32[]{:S(2)}, u32[]{:S(2)}) collective-permute-start(f32[48,8,128]{2,1,0:T(8,128)S(1)} %get-tuple-element.38), channel_id=1, source_target_pairs={{8,16},{16,8},{24,32},{32,24},{40,48},{48,40},{56,64},{64,56},{72,... | collective-permute-start | bytes 589832 | tf_op jit(solution)/shard_map/ppermute | solution.py:336
  28.5 13.3 %collective-permute-start.4 = (f32[288,128]{1,0:T(8,128)S(1)}, f32[288,128]{1,0:T(8,128)S(1)}, u32[]{:S(2)}, u32[]{:S(2)}) collective-permute-start(f32[288,128]{1,0:T(8,128)S(1)} %get-tuple-element.34), channel_id=1, source_target_pairs={{0,8},{8,0},{16,24},{24,16},{32,40},{40,32},{48,56},{56,48},{64,72... | collective-permute-start | bytes 442376 | tf_op jit(solution)/shard_map/ppermute | solution.py:336
  35.4 6.9 %collective-permute-start.5 = (f32[96,128]{1,0:T(8,128)S(1)}, f32[96,128]{1,0:T(8,128)S(1)}, u32[]{:S(2)}, u32[]{:S(2)}) collective-permute-start(f32[96,128]{1,0:T(8,128)S(1)} %get-tuple-element.37), channel_id=1, source_target_pairs={{0,8},{8,0},{16,24},{24,16},{32,40},{40,32},{48,56},{56,48},{64,72... | collective-permute-start | bytes 147464 | tf_op jit(solution)/shard_map/ppermute | solution.py:336

commit v2 on v1

--- a/solution.py
+++ b/solution.py
@@ -16,6 +16,7 @@
     0.8717401485096066,
 ]
 LANES = 128
+COMPONENTS = 3
 BLOCK = 256
 F32 = jnp.float32
 BF16 = jnp.bfloat16
@@ -59,26 +60,31 @@
     derivative, weights = gll_tables()
     eye = np.eye(8)
 
+    def doubled(table):
+        high, low = split_table(table)
+        top = np.concatenate([high, high], 1)
+        return np.concatenate([top, np.concatenate([low, np.zeros_like(low)], 1)], 0)
+
     high, low = split_table(np.concatenate([np.kron(derivative, eye), np.kron(eye, derivative)], 0))
     grad_y = np.concatenate([high, high, low], 1)
     back = (derivative * weights[:, None]).T
-    high, low = split_table(np.concatenate([np.kron(back, np.diag(weights)), np.kron(np.diag(weights), back)], 1))
-    back_y = np.concatenate([high, high, low], 1)
-    many = np.eye(BLOCK // 8)
-    grad_z = np.concatenate(split_table(np.kron(many, derivative.T)), 0)
-    back_z = np.concatenate(split_table(np.kron(many, derivative)), 0)
+    both = np.concatenate([np.kron(back, np.diag(weights)), np.kron(np.diag(weights), back)], 1)
+    back_y = doubled(both)
+    many = np.eye(LANES // 8)
+
+    def stacked(table):
+        high, low = split_table(table)
+        bottom = np.concatenate([high, np.zeros_like(low)], 1)
+        return np.concatenate([np.concatenate([high, low], 1), bottom], 0)
+
+    grad_z = stacked(np.kron(many, derivative.T))
+    back_z = stacked(np.kron(many, derivative))
     spread = np.kron(np.eye(LANES)[:, : BLOCK // 8], np.ones((1, 8))).astype(jnp.bfloat16)
     weight_z = np.tile(weights, BLOCK // 8)[None].astype(np.float32)
     plane = np.tile(np.kron(weights, weights)[:, None], (1, BLOCK)).astype(np.float32)
     return grad_y, back_y, grad_z, back_z, spread, weight_z, plane
 
 
-def x_matrices():
-    derivative, weights = gll_tables()
-    scaled = (derivative * weights[:, None]).T / weights[:, None]
-    return derivative, scaled
-
-
 def split(values):
     high = values.astype(BF16)
     return high, (values - high.astype(F32)).astype(BF16)
@@ -92,17 +98,27 @@
     return lax.broadcasted_iota(jnp.int32, (8, LANES), 1)
 
 
-def operator_block(field, factor, gy_ref, by_ref, gz_ref, bz_ref, plane):
-    forward, backward = x_matrices()
+def along_z(high, low, table):
+    rows = high.shape[0]
+    halves = []
+    for k in range(BLOCK // LANES):
+        lanes = slice(k * LANES, k * LANES + LANES)
+        halves.append(jnp.concatenate([high[:, lanes], low[:, lanes]], 1))
+    both = dot(jnp.concatenate(halves, 0), table)
+    both = both[:, :LANES] + both[:, LANES:]
+    return jnp.concatenate([both[:rows], both[rows:]], 1)
+
+
+def operator_block(field, factor, gxy_ref, bxy_ref, gz_ref, bz_ref, plane):
     count = field.shape[0] // 64
     high, low = split(field)
-    grad_z = dot(high, gz_ref[:BLOCK]) + dot(low, gz_ref[:BLOCK]) + dot(high, gz_ref[BLOCK:])
+    grad_z = along_z(high, low, gz_ref[...])
     g = [factor[k : k + 1] for k in range(6)]
     fluxes = []
-    along_y = []
+    sums = []
     for c in range(count):
         mine = slice(64 * c, 64 * c + 64)
-        both = dot(gy_ref[...], jnp.concatenate([high[mine], low[mine], high[mine]], 0))
+        both = dot(gxy_ref[...], jnp.concatenate([high[mine], low[mine], high[mine]], 0))
         gx, gy = both[:64], both[64:]
         gz = grad_z[mine]
         fx = g[0] * gx + g[3] * gy + g[4] * gz
@@ -110,12 +126,11 @@
         fz = g[4] * gx + g[5] * gy + g[2] * gz
         fluxes.append(fz)
         fh, fl = split(jnp.concatenate([fx, fy], 0))
-        along_y.append(dot(by_ref[...], jnp.concatenate([fh, fl, fh], 0)))
+        both = dot(bxy_ref[...], jnp.concatenate([fh, fl], 0))
+        sums.append(both[:64] + both[64:])
     fh, fl = split(jnp.concatenate(fluxes, 0))
-    back = dot(fh, bz_ref[:BLOCK]) + dot(fl, bz_ref[:BLOCK]) + dot(fh, bz_ref[BLOCK:])
-    return [
-        along_y[c] + plane * back[64 * c : 64 * c + 64] for c in range(count)
-    ]
+    back = along_z(fh, fl, bz_ref[...])
+    return [sums[c] + plane * back[64 * c : 64 * c + 64] for c in range(count)]
 
 
 def spread_rows(rows, spread, weight):
@@ -192,64 +207,41 @@
 ):
     components = u_ref.shape[0]
     blocks = u_ref.shape[3] // BLOCK
-
-    def body(block, carry):
-        where = pl.ds(pl.multiple_of(block * BLOCK, BLOCK), BLOCK)
+    tiles = blocks * (BLOCK // LANES)
+    lane = lax.broadcasted_iota(jnp.int32, (64, LANES), 1)
+    last, initial = lane % 8 == 7, lane % 8 == 0
+    final_lane, first_lane = lane == LANES - 1, lane == 0
+    zero = jnp.zeros((64, LANES), F32)
+    plane = plane_ref[...]
+    pending = [None] * components
+    edge = [zero] * components
+
+    def finish(c, tile, following):
+        value, after, before, previous = pending[c]
+        after = jnp.where(final_lane, following, after)
+        before = jnp.where(first_lane, previous, before)
+        change = jnp.where(last, after, jnp.where(initial, before, 0.0))
+        out_ref[c * tiles + tile] = value + change
+
+    for block in range(blocks):
+        where = slice(block * BLOCK, block * BLOCK + BLOCK)
         field = jnp.concatenate(
             [u_ref[c, :, :, where].reshape(64, BLOCK) for c in range(components)], 0
         )
-        factor = factor_ref[pl.ds(pl.multiple_of(block * 8, 8), 8), :]
-        totals = operator_block(field, factor, gy_ref, by_ref, gz_ref, bz_ref, plane_ref[...])
+        factor = factor_ref[8 * block : 8 * block + 8, :]
+        totals = operator_block(field, factor, gy_ref, by_ref, gz_ref, bz_ref, plane)
         for c in range(components):
-            out_ref[c, :, :, where] = totals[c].reshape(8, 8, BLOCK)
-        return carry
-
-    lax.fori_loop(0, blocks, body, 0, unroll=8)
-
-
-def face_kernel(
-    in_ref, za_ref, zb_ref, out_ref, xa_ref, xb_ref, ia_ref, ea_ref, yb_ref
-):
-    components = in_ref.shape[0]
-    length = in_ref.shape[3]
-    tiles = length // LANES
-    even_x, even_y, even_z = parities()
-    low, high = ordered(even_z, za_ref[...], zb_ref[...])
-    position = lax.broadcasted_iota(jnp.int32, (8, length), 1)
-    last = (position % 8 == 7) & (position != length - 1)
-    initial = (position % 8 == 0) & (position != 0)
+            for k in range(BLOCK // LANES):
+                value = totals[c][:, k * LANES : k * LANES + LANES]
+                after = pltpu.roll(value, LANES - 1, 1)
+                before = pltpu.roll(value, 1, 1)
+                tile = block * (BLOCK // LANES) + k
+                if tile:
+                    finish(c, tile - 1, after)
+                pending[c] = (value, after, before, edge[c])
+                edge[c] = before
     for c in range(components):
-        for x in range(8):
-            row = in_ref[c, x]
-            after = pltpu.roll(row, length - 1, 1)
-            before = pltpu.roll(row, 1, 1)
-            row = row + jnp.where(last, after, 0.0) + jnp.where(initial, before, 0.0)
-            slot = 8 * c + x
-            out_ref[c, x] = row
-            out_ref[c, x, :, :LANES] = row[:, :LANES] + at_lane(low, slot, 0)
-            out_ref[c, x, :, length - LANES :] = row[:, length - LANES :] + at_lane(
-                high, slot, LANES - 1
-            )
-
-    for c in range(components):
-        for t in range(tiles):
-            where = slice(t * LANES, t * LANES + LANES)
-            spot = c * tiles + t
-            first_plane = out_ref[c, 0, :, where]
-            last_plane = out_ref[c, 7, :, where]
-            xa_ref[spot] = jnp.where(even_x, last_plane, first_plane)
-            xb_ref[spot] = jnp.where(even_x, first_plane, last_plane)
-            for x in range(8):
-                first_row = out_ref[c, x, 0:1, where]
-                last_row = out_ref[c, x, 7:8, where]
-                row_a = jnp.where(even_y, last_row, first_row)
-                yb_ref[spot, x : x + 1] = jnp.where(even_y, first_row, last_row)
-                if x in (0, 7):
-                    at = 6 * t + 2 * c + x // 7
-                    ea_ref[at : at + 1] = row_a
-                else:
-                    at = 18 * t + 6 * c + x - 1
-                    ia_ref[at : at + 1] = row_a
+        finish(c, tiles - 1, zero)
 
 
 def ordered(even, first, second):
@@ -265,6 +257,38 @@
     shift = (lane_to - slot) % LANES
     moved = pltpu.roll(packed, shift, 1) if shift else packed
     return jnp.where(lane_iota() == lane_to, moved, 0.0)
+
+
+def face_kernel(
+    local_ref, za_ref, zb_ref, xa_ref, xb_ref, ia_ref, ea_ref, yb_ref, ends_ref
+):
+    tiles = local_ref.shape[0] // COMPONENTS
+    even_x, even_y, even_z = parities()
+    low, high = ordered(even_z, za_ref[...], zb_ref[...])
+    for c in range(COMPONENTS):
+        for k, (t, packed, lane_to) in enumerate(((0, low, 0), (tiles - 1, high, LANES - 1))):
+            for x in range(8):
+                rows = slice(8 * x, 8 * x + 8)
+                halo = at_lane(packed, 8 * c + x, lane_to)
+                ends_ref[2 * c + k, rows] = local_ref[c * tiles + t, rows] + halo
+
+    for c in range(COMPONENTS):
+        for t in range(tiles):
+            spot = c * tiles + t
+            ref, at = local_ref, spot
+            if t in (0, tiles - 1):
+                ref, at = ends_ref, 2 * c + (t > 0)
+            first_plane = ref[at, 0:8]
+            last_plane = ref[at, 56:64]
+            xa_ref[spot] = jnp.where(even_x, last_plane, first_plane)
+            xb_ref[spot] = jnp.where(even_x, first_plane, last_plane)
+            first_rows = ref[at, pl.ds(0, 8, stride=8)]
+            last_rows = ref[at, pl.ds(7, 8, stride=8)]
+            rows_a = jnp.where(even_y, last_rows, first_rows)
+            yb_ref[spot] = jnp.where(even_y, first_rows, last_rows)
+            ia_ref[18 * t + 6 * c : 18 * t + 6 * c + 6] = rows_a[1:7]
+            ea_ref[6 * t + 2 * c : 6 * t + 2 * c + 1] = rows_a[0:1]
+            ea_ref[6 * t + 2 * c + 1 : 6 * t + 2 * c + 2] = rows_a[7:8]
 
 
 def copy_kernel(in_ref, out_ref):
@@ -290,11 +314,12 @@
 
 
 def final_kernel(
-    local_ref, xa_ref, xb_ref, ia_ref, ea_ref, yb_ref, out_hbm, out_ref, sems
+    local_ref, za_ref, zb_ref, xa_ref, xb_ref, ia_ref, ea_ref, yb_ref, out_hbm, out_ref, sems
 ):
-    components = local_ref.shape[0]
-    tiles = local_ref.shape[3] // LANES
-    even_x, even_y, _ = parities()
+    components = out_ref.shape[0]
+    tiles = local_ref.shape[0] // components
+    even_x, even_y, even_z = parities()
+    low, high = ordered(even_z, za_ref[...], zb_ref[...])
     sublane = lax.broadcasted_iota(jnp.int32, (8, LANES), 0)
     row_a = jnp.where(even_y, 7, 0)
     row_b = 7 - row_a
@@ -306,7 +331,11 @@
             spot = c * tiles + t
             below, above = ordered(even_x, xa_ref[spot], xb_ref[spot])
             for x in range(8):
-                value = local_ref[c, x, :, where]
+                value = local_ref[spot, 8 * x : 8 * x + 8]
+                if t == 0:
+                    value = value + at_lane(low, 8 * c + x, 0)
+                if t == tiles - 1:
+                    value = value + at_lane(high, 8 * c + x, LANES - 1)
                 if x in (0, 7):
                     value = value + (above if x else below)
                     at = 6 * t + 2 * c + x // 7
@@ -366,6 +395,7 @@
     inner = (components * tiles * 6, LANES)
     edge = (components * tiles * 2, LANES)
     tile = (8, LANES)
+    flat = (components * tiles, 64, LANES)
     constants = [jnp.asarray(table) for table in tables()]
     operands = [
         pltpu.with_memory_space_constraint(operand, pltpu.HBM)
@@ -382,9 +412,11 @@
     )(*operands)
     za = exchange(loaded[-2], "gz", 0)
     zb = exchange(loaded[-1], "gz", 1)
-    (result,) = call(stiffness_kernel, [nodal.shape])(*loaded[:-2])
-    result, xa, xb, ia, ea, yb = call(
-        face_kernel, [nodal.shape, face, face, inner, edge, face]
+    (result,) = call(stiffness_kernel, [flat])(*loaded[:-2])
+    xa, xb, ia, ea, yb = call(
+        face_kernel,
+        [face, face, inner, edge, face],
+        [pltpu.VMEM((2 * components, 64, LANES), F32)],
     )(result, za, zb)
     xa = mixed_exchange(xa, 0)
     xb = mixed_exchange(xb, 1)
@@ -398,7 +430,7 @@
         [nodal.shape],
         [pltpu.VMEM(nodal.shape, F32), pltpu.SemaphoreType.DMA((components,))],
         out_specs=[hbm],
-    )(result, xa, xb, ia, ea, yb)
+    )(result, za, zb, xa, xb, ia, ea, yb)
     return result
 
 

time: 43.9 us -> 42.7 us (0.973)
  Pallas kernels: 8.18 us -> 6.98 us
    pallas_call x2, Pallas kernels: 4.73 us -> 3.57 us  [the longest x1 3.4 us: local(): result, = call(stiffness_kernel, [flat])(*loaded[:-2])]
where the time goes in v2:
time: 42.7 us; the launch traced here: 42.4 us
  starting transfers between devices  21.8 us (51%)
  waiting for transfers between devices  13.6 us (32%)
  Pallas kernels  6.98 us (16%)
    ppermute x5, starting transfers between devices, exchange(): return lax.ppermute(array, axis, pairs_from(start, lax.axis_size(axis)))  13.4 us
    ppermute x2, waiting for transfers between devices, mixed_exchange(): return lax.ppermute(array, ('gx', 'gy', 'gz'), found)  8.57 us
    ppermute x2, starting transfers between devices, mixed_exchange(): return lax.ppermute(array, ('gx', 'gy', 'gz'), found)  8.4 us
    ppermute x5, waiting for transfers between devices, exchange(): return lax.ppermute(array, axis, pairs_from(start, lax.axis_size(axis)))  5 us
    pallas_call x1, Pallas kernels, local(): result, = call(stiffness_kernel, [flat])(*loaded[:-2])  3.4 us
    pallas_call x1, Pallas kernels, local(): call(load_kernel, [nodal.shape, (8 * blocks, BLOCK)] + kept + [tile, tile...  1.99 us
    pallas_call x1, Pallas kernels, local(): call(final_kernel, [nodal.shape], [pltpu.VMEM(nodal.shape, F32), pltpu.Se...  1.3 us
  transfers between devices with their start and end apart: 7, of which 3 were waited for; matrix products, arithmetic and copies ran while one was open for 0% of the time, Pallas kernels for 8%

profile of v2, /device:TPU:208, one launch (start us, length us, event | category | flops | bytes accessed | tf_op | source)
XLA Modules:
  0.0 42.4 jit_solution(18136574634765859828)
XLA Ops:
  0.0 2.0 %shard_map.91 = (f32[3,8,8,2048]{3,2,1,0:T(8,128)S(1)}, f32[64,256]{1,0:T(8,128)S(1)}, bf16[128,192]{1,0:T(8,128)(2,1)S(1)}, bf16[128,256]{1,0:T(8,128)(2,1)S(1)...) custom-call(f32[3,8,8,2048]{3,2,1,0:T(8,128)} %u_hbm.1, ...), custom_call_target="tpu_custom_call" | custom-call | flops 1000000 | bytes 1000000 | tf_op jit(solution)/shard_map/pallas_call | solution.py:406
  2.0 1.9 %collective-permute-start = (f32[8,128]{1,0:T(8,128)S(1)}, f32[8,128]{1,0:T(8,128)S(1)}, u32[]{:S(2)}, u32[]{:S(2)}) collective-permute-start(f32[8,128]{1,0:T(8,128)S(1)} %get-tuple-element.28), channel_id=1, source_target_pairs={{0,1},{1,0},{2,3},{3,2},{4,5},{5,4},{6,7},{7,6},{8,9},{9,8},{10,11... | collective-permute-start | bytes 12296 | tf_op jit(solution)/shard_map/ppermute | solution.py:365
  3.9 0.7 %collective-permute-start.1 = (f32[8,128]{1,0:T(8,128)S(1)}, f32[8,128]{1,0:T(8,128)S(1)}, u32[]{:S(2)}, u32[]{:S(2)}) collective-permute-start(f32[8,128]{1,0:T(8,128)S(1)} %get-tuple-element.29), channel_id=1, source_target_pairs={{1,2},{2,1},{3,4},{4,3},{5,6},{6,5},{9,10},{10,9},{11,12},{12,11},... | collective-permute-start | bytes 12296 | tf_op jit(solution)/shard_map/ppermute | solution.py:365
  4.6 3.4 %shard_map.92.local_ref = f32[48,64,128]{2,1,0:T(8,128)S(1)} custom-call(f32[3,8,8,2048]{3,2,1,0:T(8,128)S(1)} %get-tuple-element.21.u_ref, f32[64,256]{1,0:T(8,128)S(1)} %get-tuple-element.22.factor_ref, bf16[128,192]{1,0:T(8,128)(2,1)S(1)} %get-tuple-element.23.gy_ref, bf16[128,256]{1,0:T(8,128)(2,1)S(1)} %get-tuple-element.24.by_ref, ...), custom_call_target="tpu_custom_call" | custom-call | flops 1000000 | bytes 1000000 | tf_op jit(solution)/shard_map/pallas_call | solution.py:415
  8.0 0.0 collective-permute-done.za_ref
  8.0 0.0 collective-permute-done.1.zb_ref
  8.0 0.2 shard_map.93
  8.2 2.2 %collective-permute-start.2 = (f32[48,8,128]{2,1,0:T(8,128)S(1)}, f32[48,8,128]{2,1,0:T(8,128)S(1)}, u32[]{:S(2)}, u32[]{:S(2)}) collective-permute-start(f32[48,8,128]{2,1,0:T(8,128)S(1)} %get-tuple-element.30), channel_id=1, source_target_pairs={{0,128},{128,0},{256,384},{384,256},{129,257},{257,129},{2,130},{1... | collective-permute-start | bytes 589832 | tf_op jit(solution)/shard_map/ppermute | solution.py:375
  10.4 6.2 %collective-permute-start.3 = (f32[48,8,128]{2,1,0:T(8,128)S(1)}, f32[48,8,128]{2,1,0:T(8,128)S(1)}, u32[]{:S(2)}, u32[]{:S(2)}) collective-permute-start(f32[48,8,128]{2,1,0:T(8,128)S(1)} %get-tuple-element.31), channel_id=1, source_target_pairs={{128,256},{256,128},{1,129},{129,1},{257,385},{385,257},{130,258},... | collective-permute-start | bytes 589832 | tf_op jit(solution)/shard_map/ppermute | solution.py:375
  16.6 0.0 collective-permute-done.2.xa_ref
  16.7 8.5 %collective-permute-done.3.xb_ref = f32[48,8,128]{2,1,0:T(8,128)S(1)} collective-permute-done((f32[48,8,128]{2,1,0:T(8,128)S(1)}, f32[48,8,128]{2,1,0:T(8,128)S(1)}, u32[]{:S(2)}, u32[]{:S(2)}) %collective-permute-start.3) | collective-permute-done | bytes 196640 | tf_op jit(solution)/shard_map/ppermute | solution.py:375
  25.2 0.1 shard_map.95
  25.3 1.9 %collective-permute-start.6 = (f32[48,8,128]{2,1,0:T(8,128)S(1)}, f32[48,8,128]{2,1,0:T(8,128)S(1)}, u32[]{:S(2)}, u32[]{:S(2)}) collective-permute-start(f32[48,8,128]{2,1,0:T(8,128)S(1)} %get-tuple-element.36), channel_id=1, source_target_pairs={{8,16},{16,8},{24,32},{32,24},{40,48},{48,40},{56,64},{64,56},{72,... | collective-permute-start | bytes 589832 | tf_op jit(solution)/shard_map/ppermute | solution.py:365
  27.2 6.9 %collective-permute-start.4 = (f32[288,128]{1,0:T(8,128)S(1)}, f32[288,128]{1,0:T(8,128)S(1)}, u32[]{:S(2)}, u32[]{:S(2)}) collective-permute-start(f32[288,128]{1,0:T(8,128)S(1)} %get-tuple-element.32), channel_id=1, source_target_pairs={{0,8},{8,0},{16,24},{24,16},{32,40},{40,32},{48,56},{56,48},{64,72... | collective-permute-start | bytes 442376 | tf_op jit(solution)/shard_map/ppermute | solution.py:365
  34.2 1.9 %collective-permute-start.5 = (f32[96,128]{1,0:T(8,128)S(1)}, f32[96,128]{1,0:T(8,128)S(1)}, u32[]{:S(2)}, u32[]{:S(2)}) collective-permute-start(f32[96,128]{1,0:T(8,128)S(1)} %get-tuple-element.35), channel_id=1, source_target_pairs={{0,8},{8,0},{16,24},{24,16},{32,40},{40,32},{48,56},{56,48},{64,72... | collective-permute-start | bytes 147464 | tf_op jit(solution)/shard_map/ppermute | solution.py:365
  36.1 4.5 %collective-permute-done.4.ia_ref = f32[288,128]{1,0:T(8,128)S(1)} collective-permute-done((f32[288,128]{1,0:T(8,128)S(1)}, f32[288,128]{1,0:T(8,128)S(1)}, u32[]{:S(2)}, u32[]{:S(2)}) %collective-permute-start.4) | collective-permute-done | bytes 147488 | tf_op jit(solution)/shard_map/ppermute | solution.py:365
  40.6 0.5 %collective-permute-done.5.ea_ref = f32[96,128]{1,0:T(8,128)S(1)} collective-permute-done((f32[96,128]{1,0:T(8,128)S(1)}, f32[96,128]{1,0:T(8,128)S(1)}, u32[]{:S(2)}, u32[]{:S(2)}) %collective-permute-start.5) | collective-permute-done | bytes 49184 | tf_op jit(solution)/shard_map/ppermute | solution.py:365
  41.1 0.0 collective-permute-done.6.yb_ref
  41.1 1.3 %shard_map.96 = f32[3,8,8,2048]{3,2,1,0:T(8,128)} custom-call(f32[48,64,128]{2,1,0:T(8,128)S(1)} %shard_map.92.local_ref, f32[8,128]{1,0:T(8,128)S(1)} %collective-permute-done.za_ref, f32[8,128]{1,0:T(8,128)S(1)} %collective-permute-done.1.zb_ref, f32[48,8,128]{2,1,0:T(8,128)S(1)} %collective-permute-done.2.xa_ref, ...), custom_call_target="tpu_custom_call" | custom-call | flops 1000000 | bytes 1000000 | tf_op jit(solution)/shard_map/pallas_call | solution.py:428
  (1 shorter events, 0.0 us)
Async XLA Ops:
  2.0 6.0 %collective-permute-start = (f32[8,128]{1,0:T(8,128)S(1)}, f32[8,128]{1,0:T(8,128)S(1)}, u32[]{:S(2)}, u32[]{:S(2)}) collective-permute-start(f32[8,128]{1,0:T(8,128)S(1)} %get-tuple-element.28), channel_id=1, source_target_pairs={{0,1},{1,0},{2,3},{3,2},{4,5},{5,4},{6,7},{7,6},{8,9},{9,8},{10,11... | collective-permute-start | bytes 12296 | tf_op jit(solution)/shard_map/ppermute | solution.py:365
  3.9 4.1 %collective-permute-start.1 = (f32[8,128]{1,0:T(8,128)S(1)}, f32[8,128]{1,0:T(8,128)S(1)}, u32[]{:S(2)}, u32[]{:S(2)}) collective-permute-start(f32[8,128]{1,0:T(8,128)S(1)} %get-tuple-element.29), channel_id=1, source_target_pairs={{1,2},{2,1},{3,4},{4,3},{5,6},{6,5},{9,10},{10,9},{11,12},{12,11},... | collective-permute-start | bytes 12296 | tf_op jit(solution)/shard_map/ppermute | solution.py:365
  8.2 8.5 %collective-permute-start.2 = (f32[48,8,128]{2,1,0:T(8,128)S(1)}, f32[48,8,128]{2,1,0:T(8,128)S(1)}, u32[]{:S(2)}, u32[]{:S(2)}) collective-permute-start(f32[48,8,128]{2,1,0:T(8,128)S(1)} %get-tuple-element.30), channel_id=1, source_target_pairs={{0,128},{128,0},{256,384},{384,256},{129,257},{257,129},{2,130},{1... | collective-permute-start | bytes 589832 | tf_op jit(solution)/shard_map/ppermute | solution.py:375
  10.4 14.7 %collective-permute-start.3 = (f32[48,8,128]{2,1,0:T(8,128)S(1)}, f32[48,8,128]{2,1,0:T(8,128)S(1)}, u32[]{:S(2)}, u32[]{:S(2)}) collective-permute-start(f32[48,8,128]{2,1,0:T(8,128)S(1)} %get-tuple-element.31), channel_id=1, source_target_pairs={{128,256},{256,128},{1,129},{129,1},{257,385},{385,257},{130,258},... | collective-permute-start | bytes 589832 | tf_op jit(solution)/shard_map/ppermute | solution.py:375
  25.3 15.8 %collective-permute-start.6 = (f32[48,8,128]{2,1,0:T(8,128)S(1)}, f32[48,8,128]{2,1,0:T(8,128)S(1)}, u32[]{:S(2)}, u32[]{:S(2)}) collective-permute-start(f32[48,8,128]{2,1,0:T(8,128)S(1)} %get-tuple-element.36), channel_id=1, source_target_pairs={{8,16},{16,8},{24,32},{32,24},{40,48},{48,40},{56,64},{64,56},{72,... | collective-permute-start | bytes 589832 | tf_op jit(solution)/shard_map/ppermute | solution.py:365
  27.2 13.3 %collective-permute-start.4 = (f32[288,128]{1,0:T(8,128)S(1)}, f32[288,128]{1,0:T(8,128)S(1)}, u32[]{:S(2)}, u32[]{:S(2)}) collective-permute-start(f32[288,128]{1,0:T(8,128)S(1)} %get-tuple-element.32), channel_id=1, source_target_pairs={{0,8},{8,0},{16,24},{24,16},{32,40},{40,32},{48,56},{56,48},{64,72... | collective-permute-start | bytes 442376 | tf_op jit(solution)/shard_map/ppermute | solution.py:365
  34.2 6.9 %collective-permute-start.5 = (f32[96,128]{1,0:T(8,128)S(1)}, f32[96,128]{1,0:T(8,128)S(1)}, u32[]{:S(2)}, u32[]{:S(2)}) collective-permute-start(f32[96,128]{1,0:T(8,128)S(1)} %get-tuple-element.35), channel_id=1, source_target_pairs={{0,8},{8,0},{16,24},{24,16},{32,40},{40,32},{48,56},{56,48},{64,72... | collective-permute-start | bytes 147464 | tf_op jit(solution)/shard_map/ppermute | solution.py:365

commit v3 on v2

--- a/solution.py
+++ b/solution.py
@@ -250,7 +250,11 @@
 
 def parities():
     x, y, z = [lax.axis_index(axis) for axis in ("gx", "gy", "gz")]
-    return [lax.rem(index, 2) == 0 for index in (x + y + z, y, z)]
+    odd = lax.rem(z, 2)
+    y = y + z + 1
+    first = lax.rem(x * (1 - odd) + y * odd, 2) == 0
+    second = lax.rem(y * (1 - odd) + x * odd, 2) == 0
+    return first, second, odd == 0
 
 
 def at_lane(packed, slot, lane_to):
@@ -260,10 +264,10 @@
 
 
 def face_kernel(
-    local_ref, za_ref, zb_ref, xa_ref, xb_ref, ia_ref, ea_ref, yb_ref, ends_ref
+    local_ref, za_ref, zb_ref, fa_ref, fb_ref, ia_ref, ea_ref, sb_ref, ends_ref
 ):
     tiles = local_ref.shape[0] // COMPONENTS
-    even_x, even_y, even_z = parities()
+    even_first, even_second, even_z = parities()
     low, high = ordered(even_z, za_ref[...], zb_ref[...])
     for c in range(COMPONENTS):
         for k, (t, packed, lane_to) in enumerate(((0, low, 0), (tiles - 1, high, LANES - 1))):
@@ -278,58 +282,57 @@
             ref, at = local_ref, spot
             if t in (0, tiles - 1):
                 ref, at = ends_ref, 2 * c + (t > 0)
-            first_plane = ref[at, 0:8]
-            last_plane = ref[at, 56:64]
-            xa_ref[spot] = jnp.where(even_x, last_plane, first_plane)
-            xb_ref[spot] = jnp.where(even_x, first_plane, last_plane)
-            first_rows = ref[at, pl.ds(0, 8, stride=8)]
-            last_rows = ref[at, pl.ds(7, 8, stride=8)]
-            rows_a = jnp.where(even_y, last_rows, first_rows)
-            yb_ref[spot] = jnp.where(even_y, first_rows, last_rows)
-            ia_ref[18 * t + 6 * c : 18 * t + 6 * c + 6] = rows_a[1:7]
-            ea_ref[6 * t + 2 * c : 6 * t + 2 * c + 1] = rows_a[0:1]
-            ea_ref[6 * t + 2 * c + 1 : 6 * t + 2 * c + 2] = rows_a[7:8]
+            planes = (ref[at, 0:8], ref[at, 56:64])
+            lines = (ref[at, pl.ds(0, 8, stride=8)], ref[at, pl.ds(7, 8, stride=8)])
+            near = [jnp.where(even_z, planes[k], lines[k]) for k in range(2)]
+            far = [jnp.where(even_z, lines[k], planes[k]) for k in range(2)]
+            fa_ref[spot], fb_ref[spot] = ordered(even_first, *near)
+            rows, sb_ref[spot] = ordered(even_second, *far)
+            ia_ref[18 * t + 6 * c : 18 * t + 6 * c + 6] = rows[1:7]
+            ea_ref[6 * t + 2 * c : 6 * t + 2 * c + 1] = rows[0:1]
+            ea_ref[6 * t + 2 * c + 1 : 6 * t + 2 * c + 2] = rows[7:8]
 
 
 def copy_kernel(in_ref, out_ref):
     out_ref[...] = in_ref[...]
 
 
-def edge_kernel(ea_ref, yb_ref, xa_ref, xb_ref, outa_ref, outb_ref):
-    tiles = ea_ref.shape[0] // 6
-    components = xa_ref.shape[0] // tiles
-    even_x, even_y, _ = parities()
-    for c in range(components):
+def edge_kernel(ea_ref, sb_ref, fa_ref, fb_ref, outa_ref, outb_ref):
+    tiles = ea_ref.shape[0] // (2 * COMPONENTS)
+    even_first, even_second, _ = parities()
+    for c in range(COMPONENTS):
         for t in range(tiles):
             spot = c * tiles + t
-            sides = ordered(even_x, xa_ref[spot], xb_ref[spot])
-            outb_ref[spot] = yb_ref[spot]
+            sides = ordered(even_first, fa_ref[spot], fb_ref[spot])
+            outb_ref[spot] = sb_ref[spot]
             for k in range(2):
                 at = 6 * t + 2 * c + k
                 at = slice(at, at + 1)
-                first, last = sides[k][0:1], sides[k][7:8]
-                outa_ref[at] = ea_ref[at] + jnp.where(even_y, last, first)
-                x = slice(7 * k, 7 * k + 1)
-                outb_ref[spot, x] = yb_ref[spot, x] + jnp.where(even_y, first, last)
+                row_a, row_b = ordered(even_second, sides[k][0:1], sides[k][7:8])
+                outa_ref[at] = ea_ref[at] + row_a
+                end = slice(7 * k, 7 * k + 1)
+                outb_ref[spot, end] = sb_ref[spot, end] + row_b
 
 
 def final_kernel(
-    local_ref, za_ref, zb_ref, xa_ref, xb_ref, ia_ref, ea_ref, yb_ref, out_hbm, out_ref, sems
+    local_ref, za_ref, zb_ref, fa_ref, fb_ref, ia_ref, ea_ref, sb_ref, out_hbm, out_ref, sems
 ):
-    components = out_ref.shape[0]
-    tiles = local_ref.shape[0] // components
-    even_x, even_y, even_z = parities()
+    tiles = local_ref.shape[0] // COMPONENTS
+    even_first, even_second, even_z = parities()
     low, high = ordered(even_z, za_ref[...], zb_ref[...])
     sublane = lax.broadcasted_iota(jnp.int32, (8, LANES), 0)
-    row_a = jnp.where(even_y, 7, 0)
-    row_b = 7 - row_a
-    is_a, is_b = sublane == row_a, sublane == row_b
     copies = []
-    for c in range(components):
+    for c in range(COMPONENTS):
         for t in range(tiles):
             where = slice(t * LANES, t * LANES + LANES)
             spot = c * tiles + t
-            below, above = ordered(even_x, xa_ref[spot], xb_ref[spot])
+            near = ordered(even_first, fa_ref[spot], fb_ref[spot])
+            outer = ea_ref[6 * t + 2 * c : 6 * t + 2 * c + 2]
+            inner = ia_ref[18 * t + 6 * c : 18 * t + 6 * c + 6]
+            side = jnp.concatenate([outer[0:1], inner, outer[1:2]], 0)
+            far = ordered(even_second, side, sb_ref[spot])
+            planes = [jnp.where(even_z, near[k], far[k]) for k in range(2)]
+            lines = [jnp.where(even_z, far[k], near[k]) for k in range(2)]
             for x in range(8):
                 value = local_ref[spot, 8 * x : 8 * x + 8]
                 if t == 0:
@@ -337,16 +340,11 @@
                 if t == tiles - 1:
                     value = value + at_lane(high, 8 * c + x, LANES - 1)
                 if x in (0, 7):
-                    value = value + (above if x else below)
-                    at = 6 * t + 2 * c + x // 7
-                    line = ea_ref[at : at + 1]
-                else:
-                    at = 18 * t + 6 * c + x - 1
-                    line = ia_ref[at : at + 1]
-                other = yb_ref[spot, x : x + 1]
-                line = jnp.broadcast_to(line, (8, LANES))
-                other = jnp.broadcast_to(other, (8, LANES))
-                change = jnp.where(is_a, line, jnp.where(is_b, other, 0.0))
+                    value = value + planes[x // 7]
+                first, last = [
+                    jnp.broadcast_to(lines[k][x : x + 1], (8, LANES)) for k in range(2)
+                ]
+                change = jnp.where(sublane == 0, first, jnp.where(sublane == 7, last, 0.0))
                 out_ref[c, x, :, where] = value + change
         copies.append(pltpu.make_async_copy(out_ref.at[c], out_hbm.at[c], sems.at[c]))
         copies[-1].start()
@@ -365,13 +363,18 @@
     return lax.ppermute(array, axis, pairs_from(start, lax.axis_size(axis)))
 
 
-def mixed_exchange(array, side):
+def mixed_exchange(array, phase, side):
     width, height, depth = [lax.axis_size(axis) for axis in ("gx", "gy", "gz")]
     found = []
-    for y in range(height):
-        for z in range(depth):
-            for i, j in pairs_from((side + y + z) % 2, width):
-                found.append(((i * height + y) * depth + z, (j * height + y) * depth + z))
+    for z in range(depth):
+        if (phase == 0) == (z % 2 == 0):
+            for y in range(height):
+                for i, j in pairs_from(side, width):
+                    found.append(((i * height + y) * depth + z, (j * height + y) * depth + z))
+        else:
+            for x in range(width):
+                for i, j in pairs_from((side + z + 1) % 2, height):
+                    found.append(((x * height + i) * depth + z, (x * height + j) * depth + z))
     return lax.ppermute(array, ("gx", "gy", "gz"), found)
 
 
@@ -413,24 +416,24 @@
     za = exchange(loaded[-2], "gz", 0)
     zb = exchange(loaded[-1], "gz", 1)
     (result,) = call(stiffness_kernel, [flat])(*loaded[:-2])
-    xa, xb, ia, ea, yb = call(
+    fa, fb, ia, ea, sb = call(
         face_kernel,
         [face, face, inner, edge, face],
         [pltpu.VMEM((2 * components, 64, LANES), F32)],
     )(result, za, zb)
-    xa = mixed_exchange(xa, 0)
-    xb = mixed_exchange(xb, 1)
-    ia = exchange(ia, "gy", 0)
+    fa = mixed_exchange(fa, 0, 0)
+    fb = mixed_exchange(fb, 0, 1)
+    ia = mixed_exchange(ia, 1, 0)
     (ea,) = call(copy_kernel, [edge])(ea)
-    ea, yb = call(edge_kernel, [edge, face])(ea, yb, xa, xb)
-    yb = exchange(yb, "gy", 1)
-    ea = exchange(ea, "gy", 0)
+    ea, sb = call(edge_kernel, [edge, face])(ea, sb, fa, fb)
+    sb = mixed_exchange(sb, 1, 1)
+    ea = mixed_exchange(ea, 1, 0)
     (result,) = call(
         final_kernel,
         [nodal.shape],
         [pltpu.VMEM(nodal.shape, F32), pltpu.SemaphoreType.DMA((components,))],
         out_specs=[hbm],
-    )(result, za, zb, xa, xb, ia, ea, yb)
+    )(result, za, zb, fa, fb, ia, ea, sb)
     return result
 
 

time: 42.7 us -> 44.3 us (1.037)
  the two profiles are of different devices: /device:TPU:208 before, /device:TPU:218 now
where the time goes in v3:
time: 44.3 us; the launch traced here: 44 us
  starting transfers between devices  23.2 us (52%)
  waiting for transfers between devices  13.6 us (31%)
  Pallas kernels  7.01 us (16%)
    ppermute x5, starting transfers between devices, mixed_exchange(): return lax.ppermute(array, ('gx', 'gy', 'gz'), found)  18.8 us
    ppermute x5, waiting for transfers between devices, mixed_exchange(): return lax.ppermute(array, ('gx', 'gy', 'gz'), found)  13.6 us
    ppermute x2, starting transfers between devices, exchange(): return lax.ppermute(array, axis, pairs_from(start, lax.axis_size(axis)))  4.47 us
    pallas_call x1, Pallas kernels, local(): result, = call(stiffness_kernel, [flat])(*loaded[:-2])  3.4 us
    pallas_call x1, Pallas kernels, local(): call(load_kernel, [nodal.shape, (8 * blocks, BLOCK)] + kept + [tile, tile...  1.99 us
    pallas_call x1, Pallas kernels, local(): call(final_kernel, [nodal.shape], [pltpu.VMEM(nodal.shape, F32), pltpu.Se...  1.33 us
  transfers between devices with their start and end apart: 7, of which 4 were waited for; matrix products, arithmetic and copies ran while one was open for 0% of the time, Pallas kernels for 8%

profile of v3, /device:TPU:218, one launch (start us, length us, event | category | flops | bytes accessed | tf_op | source)
XLA Modules:
  0.0 44.0 jit_solution(17992537267355664364)
XLA Ops:
  0.0 2.0 %shard_map.91 = (f32[3,8,8,2048]{3,2,1,0:T(8,128)S(1)}, f32[64,256]{1,0:T(8,128)S(1)}, bf16[128,192]{1,0:T(8,128)(2,1)S(1)}, bf16[128,256]{1,0:T(8,128)(2,1)S(1)...) custom-call(f32[3,8,8,2048]{3,2,1,0:T(8,128)} %u_hbm.1, ...), custom_call_target="tpu_custom_call" | custom-call | flops 1000000 | bytes 1000000 | tf_op jit(solution)/shard_map/pallas_call | solution.py:409
  2.0 1.9 %collective-permute-start = (f32[8,128]{1,0:T(8,128)S(1)}, f32[8,128]{1,0:T(8,128)S(1)}, u32[]{:S(2)}, u32[]{:S(2)}) collective-permute-start(f32[8,128]{1,0:T(8,128)S(1)} %get-tuple-element.28), channel_id=1, source_target_pairs={{0,1},{1,0},{2,3},{3,2},{4,5},{5,4},{6,7},{7,6},{8,9},{9,8},{10,11... | collective-permute-start | bytes 12296 | tf_op jit(solution)/shard_map/ppermute | solution.py:363
  3.9 2.5 %collective-permute-start.1 = (f32[8,128]{1,0:T(8,128)S(1)}, f32[8,128]{1,0:T(8,128)S(1)}, u32[]{:S(2)}, u32[]{:S(2)}) collective-permute-start(f32[8,128]{1,0:T(8,128)S(1)} %get-tuple-element.29), channel_id=1, source_target_pairs={{1,2},{2,1},{3,4},{4,3},{5,6},{6,5},{9,10},{10,9},{11,12},{12,11},... | collective-permute-start | bytes 12296 | tf_op jit(solution)/shard_map/ppermute | solution.py:363
  6.5 3.4 %shard_map.92.local_ref = f32[48,64,128]{2,1,0:T(8,128)S(1)} custom-call(f32[3,8,8,2048]{3,2,1,0:T(8,128)S(1)} %get-tuple-element.21.u_ref, f32[64,256]{1,0:T(8,128)S(1)} %get-tuple-element.22.factor_ref, bf16[128,192]{1,0:T(8,128)(2,1)S(1)} %get-tuple-element.23.gy_ref, bf16[128,256]{1,0:T(8,128)(2,1)S(1)} %get-tuple-element.24.by_ref, ...), custom_call_target="tpu_custom_call" | custom-call | flops 1000000 | bytes 1000000 | tf_op jit(solution)/shard_map/pallas_call | solution.py:418
  9.9 0.0 collective-permute-done.za_ref
  9.9 0.0 collective-permute-done.1.zb_ref
  9.9 0.2 shard_map.93
  10.1 2.2 %collective-permute-start.2 = (f32[48,8,128]{2,1,0:T(8,128)S(1)}, f32[48,8,128]{2,1,0:T(8,128)S(1)}, u32[]{:S(2)}, u32[]{:S(2)}) collective-permute-start(f32[48,8,128]{2,1,0:T(8,128)S(1)} %get-tuple-element.30), channel_id=1, source_target_pairs={{0,128},{128,0},{256,384},{384,256},{8,136},{136,8},{264,392},{392... | collective-permute-start | bytes 589832 | tf_op jit(solution)/shard_map/ppermute | solution.py:378
  12.3 5.3 %collective-permute-start.3 = (f32[48,8,128]{2,1,0:T(8,128)S(1)}, f32[48,8,128]{2,1,0:T(8,128)S(1)}, u32[]{:S(2)}, u32[]{:S(2)}) collective-permute-start(f32[48,8,128]{2,1,0:T(8,128)S(1)} %get-tuple-element.31), channel_id=1, source_target_pairs={{128,256},{256,128},{136,264},{264,136},{144,272},{272,144},{152,2... | collective-permute-start | bytes 589832 | tf_op jit(solution)/shard_map/ppermute | solution.py:378
  17.6 3.1 %collective-permute-done.2.fa_ref = f32[48,8,128]{2,1,0:T(8,128)S(1)} collective-permute-done((f32[48,8,128]{2,1,0:T(8,128)S(1)}, f32[48,8,128]{2,1,0:T(8,128)S(1)}, u32[]{:S(2)}, u32[]{:S(2)}) %collective-permute-start.2) | collective-permute-done | bytes 196640 | tf_op jit(solution)/shard_map/ppermute | solution.py:378
  20.7 4.4 %collective-permute-done.3.fb_ref = f32[48,8,128]{2,1,0:T(8,128)S(1)} collective-permute-done((f32[48,8,128]{2,1,0:T(8,128)S(1)}, f32[48,8,128]{2,1,0:T(8,128)S(1)}, u32[]{:S(2)}, u32[]{:S(2)}) %collective-permute-start.3) | collective-permute-done | bytes 196640 | tf_op jit(solution)/shard_map/ppermute | solution.py:378
  25.1 0.1 shard_map.95
  25.2 1.9 %collective-permute-start.6 = (f32[48,8,128]{2,1,0:T(8,128)S(1)}, f32[48,8,128]{2,1,0:T(8,128)S(1)}, u32[]{:S(2)}, u32[]{:S(2)}) collective-permute-start(f32[48,8,128]{2,1,0:T(8,128)S(1)} %get-tuple-element.36), channel_id=1, source_target_pairs={{0,8},{8,0},{16,24},{24,16},{32,40},{40,32},{48,56},{56,48},{64,72... | collective-permute-start | bytes 589832 | tf_op jit(solution)/shard_map/ppermute | solution.py:378
  27.1 7.4 %collective-permute-start.4 = (f32[288,128]{1,0:T(8,128)S(1)}, f32[288,128]{1,0:T(8,128)S(1)}, u32[]{:S(2)}, u32[]{:S(2)}) collective-permute-start(f32[288,128]{1,0:T(8,128)S(1)} %get-tuple-element.32), channel_id=1, source_target_pairs={{8,16},{16,8},{24,32},{32,24},{40,48},{48,40},{56,64},{64,56},{72,... | collective-permute-start | bytes 442376 | tf_op jit(solution)/shard_map/ppermute | solution.py:378
  34.5 1.9 %collective-permute-start.5 = (f32[96,128]{1,0:T(8,128)S(1)}, f32[96,128]{1,0:T(8,128)S(1)}, u32[]{:S(2)}, u32[]{:S(2)}) collective-permute-start(f32[96,128]{1,0:T(8,128)S(1)} %get-tuple-element.35), channel_id=1, source_target_pairs={{8,16},{16,8},{24,32},{32,24},{40,48},{48,40},{56,64},{64,56},{72,... | collective-permute-start | bytes 147464 | tf_op jit(solution)/shard_map/ppermute | solution.py:378
  36.5 2.5 %collective-permute-done.4.ia_ref = f32[288,128]{1,0:T(8,128)S(1)} collective-permute-done((f32[288,128]{1,0:T(8,128)S(1)}, f32[288,128]{1,0:T(8,128)S(1)}, u32[]{:S(2)}, u32[]{:S(2)}) %collective-permute-start.4) | collective-permute-done | bytes 147488 | tf_op jit(solution)/shard_map/ppermute | solution.py:378
  38.9 3.7 %collective-permute-done.5.ea_ref = f32[96,128]{1,0:T(8,128)S(1)} collective-permute-done((f32[96,128]{1,0:T(8,128)S(1)}, f32[96,128]{1,0:T(8,128)S(1)}, u32[]{:S(2)}, u32[]{:S(2)}) %collective-permute-start.5) | collective-permute-done | bytes 49184 | tf_op jit(solution)/shard_map/ppermute | solution.py:378
  42.6 0.0 collective-permute-done.6.sb_ref
  42.6 1.3 %shard_map.96 = f32[3,8,8,2048]{3,2,1,0:T(8,128)} custom-call(f32[48,64,128]{2,1,0:T(8,128)S(1)} %shard_map.92.local_ref, f32[8,128]{1,0:T(8,128)S(1)} %collective-permute-done.za_ref, f32[8,128]{1,0:T(8,128)S(1)} %collective-permute-done.1.zb_ref, f32[48,8,128]{2,1,0:T(8,128)S(1)} %collective-permute-done.2.fa_ref, ...), custom_call_target="tpu_custom_call" | custom-call | flops 1000000 | bytes 1000000 | tf_op jit(solution)/shard_map/pallas_call | solution.py:431
  (1 shorter events, 0.0 us)
Async XLA Ops:
  2.0 7.9 %collective-permute-start = (f32[8,128]{1,0:T(8,128)S(1)}, f32[8,128]{1,0:T(8,128)S(1)}, u32[]{:S(2)}, u32[]{:S(2)}) collective-permute-start(f32[8,128]{1,0:T(8,128)S(1)} %get-tuple-element.28), channel_id=1, source_target_pairs={{0,1},{1,0},{2,3},{3,2},{4,5},{5,4},{6,7},{7,6},{8,9},{9,8},{10,11... | collective-permute-start | bytes 12296 | tf_op jit(solution)/shard_map/ppermute | solution.py:363
  3.9 6.0 %collective-permute-start.1 = (f32[8,128]{1,0:T(8,128)S(1)}, f32[8,128]{1,0:T(8,128)S(1)}, u32[]{:S(2)}, u32[]{:S(2)}) collective-permute-start(f32[8,128]{1,0:T(8,128)S(1)} %get-tuple-element.29), channel_id=1, source_target_pairs={{1,2},{2,1},{3,4},{4,3},{5,6},{6,5},{9,10},{10,9},{11,12},{12,11},... | collective-permute-start | bytes 12296 | tf_op jit(solution)/shard_map/ppermute | solution.py:363
  10.1 10.6 %collective-permute-start.2 = (f32[48,8,128]{2,1,0:T(8,128)S(1)}, f32[48,8,128]{2,1,0:T(8,128)S(1)}, u32[]{:S(2)}, u32[]{:S(2)}) collective-permute-start(f32[48,8,128]{2,1,0:T(8,128)S(1)} %get-tuple-element.30), channel_id=1, source_target_pairs={{0,128},{128,0},{256,384},{384,256},{8,136},{136,8},{264,392},{392... | collective-permute-start | bytes 589832 | tf_op jit(solution)/shard_map/ppermute | solution.py:378
  12.3 12.7 %collective-permute-start.3 = (f32[48,8,128]{2,1,0:T(8,128)S(1)}, f32[48,8,128]{2,1,0:T(8,128)S(1)}, u32[]{:S(2)}, u32[]{:S(2)}) collective-permute-start(f32[48,8,128]{2,1,0:T(8,128)S(1)} %get-tuple-element.31), channel_id=1, source_target_pairs={{128,256},{256,128},{136,264},{264,136},{144,272},{272,144},{152,2... | collective-permute-start | bytes 589832 | tf_op jit(solution)/shard_map/ppermute | solution.py:378
  25.2 17.5 %collective-permute-start.6 = (f32[48,8,128]{2,1,0:T(8,128)S(1)}, f32[48,8,128]{2,1,0:T(8,128)S(1)}, u32[]{:S(2)}, u32[]{:S(2)}) collective-permute-start(f32[48,8,128]{2,1,0:T(8,128)S(1)} %get-tuple-element.36), channel_id=1, source_target_pairs={{0,8},{8,0},{16,24},{24,16},{32,40},{40,32},{48,56},{56,48},{64,72... | collective-permute-start | bytes 589832 | tf_op jit(solution)/shard_map/ppermute | solution.py:378
  27.1 11.8 %collective-permute-start.4 = (f32[288,128]{1,0:T(8,128)S(1)}, f32[288,128]{1,0:T(8,128)S(1)}, u32[]{:S(2)}, u32[]{:S(2)}) collective-permute-start(f32[288,128]{1,0:T(8,128)S(1)} %get-tuple-element.32), channel_id=1, source_target_pairs={{8,16},{16,8},{24,32},{32,24},{40,48},{48,40},{56,64},{64,56},{72,... | collective-permute-start | bytes 442376 | tf_op jit(solution)/shard_map/ppermute | solution.py:378
  34.5 8.1 %collective-permute-start.5 = (f32[96,128]{1,0:T(8,128)S(1)}, f32[96,128]{1,0:T(8,128)S(1)}, u32[]{:S(2)}, u32[]{:S(2)}) collective-permute-start(f32[96,128]{1,0:T(8,128)S(1)} %get-tuple-element.35), channel_id=1, source_target_pairs={{8,16},{16,8},{24,32},{32,24},{40,48},{48,40},{56,64},{64,56},{72,... | collective-permute-start | bytes 147464 | tf_op jit(solution)/shard_map/ppermute | solution.py:378

commit v4 on v3

--- a/solution.py
+++ b/solution.py
@@ -99,14 +99,14 @@
 
 
 def along_z(high, low, table):
-    rows = high.shape[0]
+    rows, width = high.shape
     halves = []
-    for k in range(BLOCK // LANES):
+    for k in range(width // LANES):
         lanes = slice(k * LANES, k * LANES + LANES)
         halves.append(jnp.concatenate([high[:, lanes], low[:, lanes]], 1))
     both = dot(jnp.concatenate(halves, 0), table)
     both = both[:, :LANES] + both[:, LANES:]
-    return jnp.concatenate([both[:rows], both[rows:]], 1)
+    return jnp.concatenate([both[k * rows : k * rows + rows] for k in range(width // LANES)], 1)
 
 
 def operator_block(field, factor, gxy_ref, bxy_ref, gz_ref, bz_ref, plane):
@@ -176,12 +176,15 @@
     factor_ref[...] = expanded
     for copy in copies[3:10]:
         copy.wait()
-    factor = jnp.concatenate([expanded[:8, :LANES], expanded[8 * blocks - 8 :, LANES:]], 1)
+    lower = lane_iota() < LANES // 2
+    factor = jnp.where(lower, expanded[:8, :LANES], expanded[8 * blocks - 8 :, LANES:])
+    lower = lax.broadcasted_iota(jnp.int32, (64, LANES), 1) < LANES // 2
     sides = []
     for c in range(components):
-        sides.append(jnp.concatenate([u_ref[c, :, :, where].reshape(64, LANES) for where in ends], 1))
+        begin, end = [u_ref[c, :, :, where].reshape(64, LANES) for where in ends]
+        sides.append(jnp.where(lower, begin, end))
     totals = operator_block(
-        jnp.concatenate(sides, 0), factor, gy_ref, by_ref, gz_ref, bz_ref, plane_ref[...]
+        jnp.concatenate(sides, 0), factor, gy_ref, by_ref, gz_ref, bz_ref, plane_ref[:, :LANES]
     )
     even_z = lax.rem(lax.axis_index("gz"), 2) == 0
     lane = lane_iota()
@@ -190,10 +193,9 @@
     for c in range(components):
         for x in range(8):
             slot = 8 * c + x
-            begin = totals[c][8 * x : 8 * x + 8, :LANES]
-            end = totals[c][8 * x : 8 * x + 8, LANES:]
-            begin = pltpu.roll(begin, slot, 1) if slot else begin
-            end = pltpu.roll(end, slot + 1, 1)
+            both = totals[c][8 * x : 8 * x + 8]
+            begin = pltpu.roll(both, slot, 1) if slot else both
+            end = pltpu.roll(both, slot + 1, 1)
             low_plane = jnp.where(lane == slot, begin, low_plane)
             high_plane = jnp.where(lane == slot, end, high_plane)
     za_ref[...] = jnp.where(even_z, high_plane, low_plane)
@@ -250,11 +252,7 @@
 
 def parities():
     x, y, z = [lax.axis_index(axis) for axis in ("gx", "gy", "gz")]
-    odd = lax.rem(z, 2)
-    y = y + z + 1
-    first = lax.rem(x * (1 - odd) + y * odd, 2) == 0
-    second = lax.rem(y * (1 - odd) + x * odd, 2) == 0
-    return first, second, odd == 0
+    return [lax.rem(index, 2) == 0 for index in (x + z, y + z, z)]
 
 
 def at_lane(packed, slot, lane_to):
@@ -267,7 +265,7 @@
     local_ref, za_ref, zb_ref, fa_ref, fb_ref, ia_ref, ea_ref, sb_ref, ends_ref
 ):
     tiles = local_ref.shape[0] // COMPONENTS
-    even_first, even_second, even_z = parities()
+    even_x, even_y, even_z = parities()
     low, high = ordered(even_z, za_ref[...], zb_ref[...])
     for c in range(COMPONENTS):
         for k, (t, packed, lane_to) in enumerate(((0, low, 0), (tiles - 1, high, LANES - 1))):
@@ -282,15 +280,12 @@
             ref, at = local_ref, spot
             if t in (0, tiles - 1):
                 ref, at = ends_ref, 2 * c + (t > 0)
-            planes = (ref[at, 0:8], ref[at, 56:64])
             lines = (ref[at, pl.ds(0, 8, stride=8)], ref[at, pl.ds(7, 8, stride=8)])
-            near = [jnp.where(even_z, planes[k], lines[k]) for k in range(2)]
-            far = [jnp.where(even_z, lines[k], planes[k]) for k in range(2)]
-            fa_ref[spot], fb_ref[spot] = ordered(even_first, *near)
-            rows, sb_ref[spot] = ordered(even_second, *far)
-            ia_ref[18 * t + 6 * c : 18 * t + 6 * c + 6] = rows[1:7]
-            ea_ref[6 * t + 2 * c : 6 * t + 2 * c + 1] = rows[0:1]
-            ea_ref[6 * t + 2 * c + 1 : 6 * t + 2 * c + 2] = rows[7:8]
+            fa_ref[spot], fb_ref[spot] = ordered(even_y, *lines)
+            plane, sb_ref[spot] = ordered(even_x, ref[at, 0:8], ref[at, 56:64])
+            ia_ref[18 * t + 6 * c : 18 * t + 6 * c + 6] = plane[1:7]
+            ea_ref[6 * t + 2 * c : 6 * t + 2 * c + 1] = plane[0:1]
+            ea_ref[6 * t + 2 * c + 1 : 6 * t + 2 * c + 2] = plane[7:8]
 
 
 def copy_kernel(in_ref, out_ref):
@@ -299,26 +294,26 @@
 
 def edge_kernel(ea_ref, sb_ref, fa_ref, fb_ref, outa_ref, outb_ref):
     tiles = ea_ref.shape[0] // (2 * COMPONENTS)
-    even_first, even_second, _ = parities()
+    even_x, even_y, _ = parities()
     for c in range(COMPONENTS):
         for t in range(tiles):
             spot = c * tiles + t
-            sides = ordered(even_first, fa_ref[spot], fb_ref[spot])
+            sides = ordered(even_y, fa_ref[spot], fb_ref[spot])
             outb_ref[spot] = sb_ref[spot]
             for k in range(2):
                 at = 6 * t + 2 * c + k
                 at = slice(at, at + 1)
-                row_a, row_b = ordered(even_second, sides[k][0:1], sides[k][7:8])
+                row_a, row_b = ordered(even_x, sides[k][0:1], sides[k][7:8])
                 outa_ref[at] = ea_ref[at] + row_a
                 end = slice(7 * k, 7 * k + 1)
                 outb_ref[spot, end] = sb_ref[spot, end] + row_b
 
 
-def final_kernel(
-    local_ref, za_ref, zb_ref, fa_ref, fb_ref, ia_ref, ea_ref, sb_ref, out_hbm, out_ref, sems
+def base_kernel(
+    local_ref, za_ref, zb_ref, fa_ref, fb_ref, out_hbm, first_ref, last_ref, out_ref, sems
 ):
     tiles = local_ref.shape[0] // COMPONENTS
-    even_first, even_second, even_z = parities()
+    _, even_y, even_z = parities()
     low, high = ordered(even_z, za_ref[...], zb_ref[...])
     sublane = lax.broadcasted_iota(jnp.int32, (8, LANES), 0)
     copies = []
@@ -326,28 +321,53 @@
         for t in range(tiles):
             where = slice(t * LANES, t * LANES + LANES)
             spot = c * tiles + t
-            near = ordered(even_first, fa_ref[spot], fb_ref[spot])
-            outer = ea_ref[6 * t + 2 * c : 6 * t + 2 * c + 2]
-            inner = ia_ref[18 * t + 6 * c : 18 * t + 6 * c + 6]
-            side = jnp.concatenate([outer[0:1], inner, outer[1:2]], 0)
-            far = ordered(even_second, side, sb_ref[spot])
-            planes = [jnp.where(even_z, near[k], far[k]) for k in range(2)]
-            lines = [jnp.where(even_z, far[k], near[k]) for k in range(2)]
+            lines = ordered(even_y, fa_ref[spot], fb_ref[spot])
             for x in range(8):
                 value = local_ref[spot, 8 * x : 8 * x + 8]
                 if t == 0:
                     value = value + at_lane(low, 8 * c + x, 0)
                 if t == tiles - 1:
                     value = value + at_lane(high, 8 * c + x, LANES - 1)
-                if x in (0, 7):
-                    value = value + planes[x // 7]
                 first, last = [
                     jnp.broadcast_to(lines[k][x : x + 1], (8, LANES)) for k in range(2)
                 ]
                 change = jnp.where(sublane == 0, first, jnp.where(sublane == 7, last, 0.0))
-                out_ref[c, x, :, where] = value + change
-        copies.append(pltpu.make_async_copy(out_ref.at[c], out_hbm.at[c], sems.at[c]))
+                if x == 0:
+                    first_ref[spot] = value + change
+                elif x == 7:
+                    last_ref[spot] = value + change
+                else:
+                    out_ref[c, x - 1, :, where] = value + change
+        copies.append(pltpu.make_async_copy(out_ref.at[c], out_hbm.at[c, 1:7], sems.at[c]))
         copies[-1].start()
+    for copy in copies:
+        copy.wait()
+
+
+def late_kernel(
+    base_hbm, first_ref, last_ref, ia_ref, ea_ref, sb_ref, out_hbm, planes_ref, sems
+):
+    del base_hbm
+    tiles = first_ref.shape[0] // COMPONENTS
+    even_x, _, _ = parities()
+    copies = []
+    for c in range(COMPONENTS):
+        for t in range(tiles):
+            where = slice(t * LANES, t * LANES + LANES)
+            spot = c * tiles + t
+            outer = ea_ref[6 * t + 2 * c : 6 * t + 2 * c + 2]
+            inner = ia_ref[18 * t + 6 * c : 18 * t + 6 * c + 6]
+            side = jnp.concatenate([outer[0:1], inner, outer[1:2]], 0)
+            below, above = ordered(even_x, side, sb_ref[spot])
+            planes_ref[c, 0, :, where] = first_ref[spot] + below
+            planes_ref[c, 1, :, where] = last_ref[spot] + above
+        for k in range(2):
+            copies.append(
+                pltpu.make_async_copy(
+                    planes_ref.at[c, k], out_hbm.at[c, 7 * k], sems.at[2 * c + k]
+                )
+            )
+            copies[-1].start()
     for copy in copies:
         copy.wait()
 
@@ -363,19 +383,13 @@
     return lax.ppermute(array, axis, pairs_from(start, lax.axis_size(axis)))
 
 
-def mixed_exchange(array, phase, side):
-    width, height, depth = [lax.axis_size(axis) for axis in ("gx", "gy", "gz")]
+def mixed_exchange(array, axis, side):
+    depth = lax.axis_size("gz")
     found = []
     for z in range(depth):
-        if (phase == 0) == (z % 2 == 0):
-            for y in range(height):
-                for i, j in pairs_from(side, width):
-                    found.append(((i * height + y) * depth + z, (j * height + y) * depth + z))
-        else:
-            for x in range(width):
-                for i, j in pairs_from((side + z + 1) % 2, height):
-                    found.append(((x * height + i) * depth + z, (x * height + j) * depth + z))
-    return lax.ppermute(array, ("gx", "gy", "gz"), found)
+        for i, j in pairs_from((side + z) % 2, lax.axis_size(axis)):
+            found.append((i * depth + z, j * depth + z))
+    return lax.ppermute(array, (axis, "gz"), found)
 
 
 def call(kernel, outs, scratch=(), flops=1000000, **specs):
@@ -421,19 +435,28 @@
         [face, face, inner, edge, face],
         [pltpu.VMEM((2 * components, 64, LANES), F32)],
     )(result, za, zb)
-    fa = mixed_exchange(fa, 0, 0)
-    fb = mixed_exchange(fb, 0, 1)
-    ia = mixed_exchange(ia, 1, 0)
+    fa = mixed_exchange(fa, "gy", 0)
+    fb = mixed_exchange(fb, "gy", 1)
+    ia = mixed_exchange(ia, "gx", 0)
     (ea,) = call(copy_kernel, [edge])(ea)
     ea, sb = call(edge_kernel, [edge, face])(ea, sb, fa, fb)
-    sb = mixed_exchange(sb, 1, 1)
-    ea = mixed_exchange(ea, 1, 0)
+    sb = mixed_exchange(sb, "gx", 1)
+    ea = mixed_exchange(ea, "gx", 0)
+    vmem = pl.BlockSpec(memory_space=pltpu.VMEM)
+    result, first, last = call(
+        base_kernel,
+        [nodal.shape, face, face],
+        [pltpu.VMEM((components, 6, 8, length), F32), pltpu.SemaphoreType.DMA((3,))],
+        out_specs=[hbm, vmem, vmem],
+    )(result, za, zb, fa, fb)
     (result,) = call(
-        final_kernel,
+        late_kernel,
         [nodal.shape],
-        [pltpu.VMEM(nodal.shape, F32), pltpu.SemaphoreType.DMA((components,))],
+        [pltpu.VMEM((components, 2, 8, length), F32), pltpu.SemaphoreType.DMA((6,))],
+        in_specs=[hbm] + [vmem] * 5,
         out_specs=[hbm],
-    )(result, za, zb, fa, fb, ia, ea, sb)
+        input_output_aliases={0: 0},
+    )(result, first, last, ia, ea, sb)
     return result
 
 

time: 44.3 us -> 44 us (level)
  the two profiles are of different devices: /device:TPU:218 before, /device:TPU:202 now
where the time goes in v4:
time: 44 us; the launch traced here: 43.7 us
  starting transfers between devices  25 us (57%)
  waiting for transfers between devices  10.8 us (25%)
  Pallas kernels  7.76 us (18%)
    ppermute x5, starting transfers between devices, mixed_exchange(): return lax.ppermute(array, (axis, 'gz'), found)  20.5 us
    ppermute x5, waiting for transfers between devices, mixed_exchange(): return lax.ppermute(array, (axis, 'gz'), found)  10.8 us
    ppermute x2, starting transfers between devices, exchange(): return lax.ppermute(array, axis, pairs_from(start, lax.axis_size(axis)))  4.47 us
    pallas_call x1, Pallas kernels, local(): result, = call(stiffness_kernel, [flat])(*loaded[:-2])  3.4 us
    pallas_call x1, Pallas kernels, local(): call(load_kernel, [nodal.shape, (8 * blocks, BLOCK)] + kept + [tile, tile...  1.84 us
    pallas_call x1, Pallas kernels, local(): call(base_kernel, [nodal.shape, face, face], [pltpu.VMEM((components, 6,...  1.41 us
  transfers between devices with their start and end apart: 7, of which 2 were waited for; matrix products, arithmetic and copies ran while one was open for 0% of the time, Pallas kernels for 11%

profile of v4, /device:TPU:202, one launch (start us, length us, event | category | flops | bytes accessed | tf_op | source)
XLA Modules:
  0.0 43.7 jit_solution(4907677506853225854)
XLA Ops:
  0.0 1.8 %shard_map.91 = (f32[3,8,8,2048]{3,2,1,0:T(8,128)S(1)}, f32[64,256]{1,0:T(8,128)S(1)}, bf16[128,192]{1,0:T(8,128)(2,1)S(1)}, bf16[128,256]{1,0:T(8,128)(2,1)S(1)...) custom-call(f32[3,8,8,2048]{3,2,1,0:T(8,128)} %u_hbm.1, ...), custom_call_target="tpu_custom_call" | custom-call | flops 1000000 | bytes 1000000 | tf_op jit(solution)/shard_map/pallas_call | solution.py:423
  1.8 1.9 %collective-permute-start = (f32[8,128]{1,0:T(8,128)S(1)}, f32[8,128]{1,0:T(8,128)S(1)}, u32[]{:S(2)}, u32[]{:S(2)}) collective-permute-start(f32[8,128]{1,0:T(8,128)S(1)} %get-tuple-element.31), channel_id=1, source_target_pairs={{0,1},{1,0},{2,3},{3,2},{4,5},{5,4},{6,7},{7,6},{8,9},{9,8},{10,11... | collective-permute-start | bytes 12296 | tf_op jit(solution)/shard_map/ppermute | solution.py:383
  3.8 2.5 %collective-permute-start.1 = (f32[8,128]{1,0:T(8,128)S(1)}, f32[8,128]{1,0:T(8,128)S(1)}, u32[]{:S(2)}, u32[]{:S(2)}) collective-permute-start(f32[8,128]{1,0:T(8,128)S(1)} %get-tuple-element.32), channel_id=1, source_target_pairs={{1,2},{2,1},{3,4},{4,3},{5,6},{6,5},{9,10},{10,9},{11,12},{12,11},... | collective-permute-start | bytes 12296 | tf_op jit(solution)/shard_map/ppermute | solution.py:383
  6.3 3.4 %shard_map.92.local_ref = f32[48,64,128]{2,1,0:T(8,128)S(1)} custom-call(f32[3,8,8,2048]{3,2,1,0:T(8,128)S(1)} %get-tuple-element.24.u_ref, f32[64,256]{1,0:T(8,128)S(1)} %get-tuple-element.25.factor_ref, bf16[128,192]{1,0:T(8,128)(2,1)S(1)} %get-tuple-element.26.gy_ref, bf16[128,256]{1,0:T(8,128)(2,1)S(1)} %get-tuple-element.27.by_ref, ...), custom_call_target="tpu_custom_call" | custom-call | flops 1000000 | bytes 1000000 | tf_op jit(solution)/shard_map/pallas_call | solution.py:432
  9.7 0.0 collective-permute-done.za_ref
  9.7 0.0 collective-permute-done.1.zb_ref
  9.8 0.2 shard_map.93
  9.9 2.4 %collective-permute-start.2 = (f32[48,8,128]{2,1,0:T(8,128)S(1)}, f32[48,8,128]{2,1,0:T(8,128)S(1)}, u32[]{:S(2)}, u32[]{:S(2)}) collective-permute-start(f32[48,8,128]{2,1,0:T(8,128)S(1)} %get-tuple-element.33), channel_id=1, source_target_pairs={{0,8},{8,0},{16,24},{24,16},{32,40},{40,32},{48,56},{56,48},{64,72... | collective-permute-start | bytes 589832 | tf_op jit(solution)/shard_map/ppermute | solution.py:392
  12.3 6.5 %collective-permute-start.3 = (f32[48,8,128]{2,1,0:T(8,128)S(1)}, f32[48,8,128]{2,1,0:T(8,128)S(1)}, u32[]{:S(2)}, u32[]{:S(2)}) collective-permute-start(f32[48,8,128]{2,1,0:T(8,128)S(1)} %get-tuple-element.34), channel_id=1, source_target_pairs={{8,16},{16,8},{24,32},{32,24},{40,48},{48,40},{56,64},{64,56},{72,... | collective-permute-start | bytes 589832 | tf_op jit(solution)/shard_map/ppermute | solution.py:392
  18.8 0.0 collective-permute-done.2.fa_ref
  18.8 7.1 %collective-permute-done.3.fb_ref = f32[48,8,128]{2,1,0:T(8,128)S(1)} collective-permute-done((f32[48,8,128]{2,1,0:T(8,128)S(1)}, f32[48,8,128]{2,1,0:T(8,128)S(1)}, u32[]{:S(2)}, u32[]{:S(2)}) %collective-permute-start.3) | collective-permute-done | bytes 196640 | tf_op jit(solution)/shard_map/ppermute | solution.py:392
  25.9 0.1 shard_map.96
  26.0 0.7 %collective-permute-start.6 = (f32[48,8,128]{2,1,0:T(8,128)S(1)}, f32[48,8,128]{2,1,0:T(8,128)S(1)}, u32[]{:S(2)}, u32[]{:S(2)}) collective-permute-start(f32[48,8,128]{2,1,0:T(8,128)S(1)} %get-tuple-element.42), channel_id=1, source_target_pairs={{128,256},{256,128},{1,129},{129,1},{257,385},{385,257},{130,258},... | collective-permute-start | bytes 589832 | tf_op jit(solution)/shard_map/ppermute | solution.py:392
  26.7 9.1 %collective-permute-start.4 = (f32[288,128]{1,0:T(8,128)S(1)}, f32[288,128]{1,0:T(8,128)S(1)}, u32[]{:S(2)}, u32[]{:S(2)}) collective-permute-start(f32[288,128]{1,0:T(8,128)S(1)} %get-tuple-element.38), channel_id=1, source_target_pairs={{0,128},{128,0},{256,384},{384,256},{129,257},{257,129},{2,130},{1... | collective-permute-start | bytes 442376 | tf_op jit(solution)/shard_map/ppermute | solution.py:392
  35.8 1.9 %collective-permute-start.5 = (f32[96,128]{1,0:T(8,128)S(1)}, f32[96,128]{1,0:T(8,128)S(1)}, u32[]{:S(2)}, u32[]{:S(2)}) collective-permute-start(f32[96,128]{1,0:T(8,128)S(1)} %get-tuple-element.41), channel_id=1, source_target_pairs={{0,128},{128,0},{256,384},{384,256},{129,257},{257,129},{2,130},{1... | collective-permute-start | bytes 147464 | tf_op jit(solution)/shard_map/ppermute | solution.py:392
  37.7 1.4 %shard_map.94 = (f32[3,8,8,2048]{3,2,1,0:T(8,128)}, f32[48,8,128]{2,1,0:T(8,128)S(1)}, f32[48,8,128]{2,1,0:T(8,128)S(1)}) custom-call(f32[48,64,128]{2,1,0:T(8,128)S(1)} %shard_map.92.local_ref, f32[8,128]{1,0:T(8,128)S(1)} %collective-permute-done.za_ref, f32[8,128]{1,0:T(8,128)S(1)} %collective-permute-done.1.zb_ref, ...), custom_call_target="tpu_custom_call" | custom-call | flops 1000000 | bytes 1000000 | tf_op jit(solution)/shard_map/pallas_call | solution.py:446
  39.2 0.0 collective-permute-done.4.ia_ref
  39.2 3.7 %collective-permute-done.5.ea_ref = f32[96,128]{1,0:T(8,128)S(1)} collective-permute-done((f32[96,128]{1,0:T(8,128)S(1)}, f32[96,128]{1,0:T(8,128)S(1)}, u32[]{:S(2)}, u32[]{:S(2)}) %collective-permute-start.5) | collective-permute-done | bytes 49184 | tf_op jit(solution)/shard_map/ppermute | solution.py:392
  42.9 0.0 collective-permute-done.6.sb_ref
  42.9 0.8 %shard_map.97 = f32[3,8,8,2048]{3,2,1,0:T(8,128)} custom-call(f32[3,8,8,2048]{3,2,1,0:T(8,128)} %get-tuple-element.35.base_hbm, f32[48,8,128]{2,1,0:T(8,128)S(1)} %get-tuple-element.36.first_ref, f32[48,8,128]{2,1,0:T(8,128)S(1)} %get-tuple-element.37.last_ref, f32[288,128]{1,0:T(8,128)S(1)} %collective-permute-done.4.ia_ref, ...), custom_call_target="tpu_custom_call", output_to_operand_aliasing={{}: (0, {})} | custom-call | flops 1000000 | bytes 1000000 | tf_op jit(solution)/shard_map/pallas_call | solution.py:452
  (1 shorter events, 0.0 us)
Async XLA Ops:
  1.8 7.9 %collective-permute-start = (f32[8,128]{1,0:T(8,128)S(1)}, f32[8,128]{1,0:T(8,128)S(1)}, u32[]{:S(2)}, u32[]{:S(2)}) collective-permute-start(f32[8,128]{1,0:T(8,128)S(1)} %get-tuple-element.31), channel_id=1, source_target_pairs={{0,1},{1,0},{2,3},{3,2},{4,5},{5,4},{6,7},{7,6},{8,9},{9,8},{10,11... | collective-permute-start | bytes 12296 | tf_op jit(solution)/shard_map/ppermute | solution.py:383
  3.8 6.0 %collective-permute-start.1 = (f32[8,128]{1,0:T(8,128)S(1)}, f32[8,128]{1,0:T(8,128)S(1)}, u32[]{:S(2)}, u32[]{:S(2)}) collective-permute-start(f32[8,128]{1,0:T(8,128)S(1)} %get-tuple-element.32), channel_id=1, source_target_pairs={{1,2},{2,1},{3,4},{4,3},{5,6},{6,5},{9,10},{10,9},{11,12},{12,11},... | collective-permute-start | bytes 12296 | tf_op jit(solution)/shard_map/ppermute | solution.py:383
  9.9 8.9 %collective-permute-start.2 = (f32[48,8,128]{2,1,0:T(8,128)S(1)}, f32[48,8,128]{2,1,0:T(8,128)S(1)}, u32[]{:S(2)}, u32[]{:S(2)}) collective-permute-start(f32[48,8,128]{2,1,0:T(8,128)S(1)} %get-tuple-element.33), channel_id=1, source_target_pairs={{0,8},{8,0},{16,24},{24,16},{32,40},{40,32},{48,56},{56,48},{64,72... | collective-permute-start | bytes 589832 | tf_op jit(solution)/shard_map/ppermute | solution.py:392
  12.3 13.6 %collective-permute-start.3 = (f32[48,8,128]{2,1,0:T(8,128)S(1)}, f32[48,8,128]{2,1,0:T(8,128)S(1)}, u32[]{:S(2)}, u32[]{:S(2)}) collective-permute-start(f32[48,8,128]{2,1,0:T(8,128)S(1)} %get-tuple-element.34), channel_id=1, source_target_pairs={{8,16},{16,8},{24,32},{32,24},{40,48},{48,40},{56,64},{64,56},{72,... | collective-permute-start | bytes 589832 | tf_op jit(solution)/shard_map/ppermute | solution.py:392
  26.0 16.8 %collective-permute-start.6 = (f32[48,8,128]{2,1,0:T(8,128)S(1)}, f32[48,8,128]{2,1,0:T(8,128)S(1)}, u32[]{:S(2)}, u32[]{:S(2)}) collective-permute-start(f32[48,8,128]{2,1,0:T(8,128)S(1)} %get-tuple-element.42), channel_id=1, source_target_pairs={{128,256},{256,128},{1,129},{129,1},{257,385},{385,257},{130,258},... | collective-permute-start | bytes 589832 | tf_op jit(solution)/shard_map/ppermute | solution.py:392
  26.7 12.4 %collective-permute-start.4 = (f32[288,128]{1,0:T(8,128)S(1)}, f32[288,128]{1,0:T(8,128)S(1)}, u32[]{:S(2)}, u32[]{:S(2)}) collective-permute-start(f32[288,128]{1,0:T(8,128)S(1)} %get-tuple-element.38), channel_id=1, source_target_pairs={{0,128},{128,0},{256,384},{384,256},{129,257},{257,129},{2,130},{1... | collective-permute-start | bytes 442376 | tf_op jit(solution)/shard_map/ppermute | solution.py:392
  35.8 7.0 %collective-permute-start.5 = (f32[96,128]{1,0:T(8,128)S(1)}, f32[96,128]{1,0:T(8,128)S(1)}, u32[]{:S(2)}, u32[]{:S(2)}) collective-permute-start(f32[96,128]{1,0:T(8,128)S(1)} %get-tuple-element.41), channel_id=1, source_target_pairs={{0,128},{128,0},{256,384},{384,256},{129,257},{257,129},{2,130},{1... | collective-permute-start | bytes 147464 | tf_op jit(solution)/shard_map/ppermute | solution.py:392

commit v5 on v4

--- a/solution.py
+++ b/solution.py
@@ -262,7 +262,7 @@
 
 
 def face_kernel(
-    local_ref, za_ref, zb_ref, fa_ref, fb_ref, ia_ref, ea_ref, sb_ref, ends_ref
+    local_ref, za_ref, zb_ref, xa_ref, xb_ref, ya_ref, yb_ref, ends_ref
 ):
     tiles = local_ref.shape[0] // COMPONENTS
     even_x, even_y, even_z = parities()
@@ -280,40 +280,29 @@
             ref, at = local_ref, spot
             if t in (0, tiles - 1):
                 ref, at = ends_ref, 2 * c + (t > 0)
+            xa_ref[spot], xb_ref[spot] = ordered(even_x, ref[at, 0:8], ref[at, 56:64])
             lines = (ref[at, pl.ds(0, 8, stride=8)], ref[at, pl.ds(7, 8, stride=8)])
-            fa_ref[spot], fb_ref[spot] = ordered(even_y, *lines)
-            plane, sb_ref[spot] = ordered(even_x, ref[at, 0:8], ref[at, 56:64])
-            ia_ref[18 * t + 6 * c : 18 * t + 6 * c + 6] = plane[1:7]
-            ea_ref[6 * t + 2 * c : 6 * t + 2 * c + 1] = plane[0:1]
-            ea_ref[6 * t + 2 * c + 1 : 6 * t + 2 * c + 2] = plane[7:8]
-
-
-def copy_kernel(in_ref, out_ref):
-    out_ref[...] = in_ref[...]
-
-
-def edge_kernel(ea_ref, sb_ref, fa_ref, fb_ref, outa_ref, outb_ref):
-    tiles = ea_ref.shape[0] // (2 * COMPONENTS)
+            ya_ref[spot], yb_ref[spot] = ordered(even_y, *lines)
+
+
+def edge_kernel(ya_ref, yb_ref, xa_ref, xb_ref, outa_ref, outb_ref):
     even_x, even_y, _ = parities()
-    for c in range(COMPONENTS):
-        for t in range(tiles):
-            spot = c * tiles + t
-            sides = ordered(even_y, fa_ref[spot], fb_ref[spot])
-            outb_ref[spot] = sb_ref[spot]
-            for k in range(2):
-                at = 6 * t + 2 * c + k
-                at = slice(at, at + 1)
-                row_a, row_b = ordered(even_x, sides[k][0:1], sides[k][7:8])
-                outa_ref[at] = ea_ref[at] + row_a
-                end = slice(7 * k, 7 * k + 1)
-                outb_ref[spot, end] = sb_ref[spot, end] + row_b
-
-
-def base_kernel(
-    local_ref, za_ref, zb_ref, fa_ref, fb_ref, out_hbm, first_ref, last_ref, out_ref, sems
+    for spot in range(xa_ref.shape[0]):
+        sides = ordered(even_x, xa_ref[spot], xb_ref[spot])
+        outa_ref[spot] = ya_ref[spot]
+        outb_ref[spot] = yb_ref[spot]
+        for k in range(2):
+            row_a, row_b = ordered(even_y, sides[k][0:1], sides[k][7:8])
+            end = slice(7 * k, 7 * k + 1)
+            outa_ref[spot, end] = ya_ref[spot, end] + row_a
+            outb_ref[spot, end] = yb_ref[spot, end] + row_b
+
+
+def final_kernel(
+    local_ref, za_ref, zb_ref, xa_ref, xb_ref, ya_ref, yb_ref, out_hbm, out_ref, sems
 ):
     tiles = local_ref.shape[0] // COMPONENTS
-    _, even_y, even_z = parities()
+    even_x, even_y, even_z = parities()
     low, high = ordered(even_z, za_ref[...], zb_ref[...])
     sublane = lax.broadcasted_iota(jnp.int32, (8, LANES), 0)
     copies = []
@@ -321,53 +310,23 @@
         for t in range(tiles):
             where = slice(t * LANES, t * LANES + LANES)
             spot = c * tiles + t
-            lines = ordered(even_y, fa_ref[spot], fb_ref[spot])
+            planes = ordered(even_x, xa_ref[spot], xb_ref[spot])
+            lines = ordered(even_y, ya_ref[spot], yb_ref[spot])
             for x in range(8):
                 value = local_ref[spot, 8 * x : 8 * x + 8]
                 if t == 0:
                     value = value + at_lane(low, 8 * c + x, 0)
                 if t == tiles - 1:
                     value = value + at_lane(high, 8 * c + x, LANES - 1)
+                if x in (0, 7):
+                    value = value + planes[x // 7]
                 first, last = [
                     jnp.broadcast_to(lines[k][x : x + 1], (8, LANES)) for k in range(2)
                 ]
                 change = jnp.where(sublane == 0, first, jnp.where(sublane == 7, last, 0.0))
-                if x == 0:
-                    first_ref[spot] = value + change
-                elif x == 7:
-                    last_ref[spot] = value + change
-                else:
-                    out_ref[c, x - 1, :, where] = value + change
-        copies.append(pltpu.make_async_copy(out_ref.at[c], out_hbm.at[c, 1:7], sems.at[c]))
+                out_ref[c, x, :, where] = value + change
+        copies.append(pltpu.make_async_copy(out_ref.at[c], out_hbm.at[c], sems.at[c]))
         copies[-1].start()
-    for copy in copies:
-        copy.wait()
-
-
-def late_kernel(
-    base_hbm, first_ref, last_ref, ia_ref, ea_ref, sb_ref, out_hbm, planes_ref, sems
-):
-    del base_hbm
-    tiles = first_ref.shape[0] // COMPONENTS
-    even_x, _, _ = parities()
-    copies = []
-    for c in range(COMPONENTS):
-        for t in range(tiles):
-            where = slice(t * LANES, t * LANES + LANES)
-            spot = c * tiles + t
-            outer = ea_ref[6 * t + 2 * c : 6 * t + 2 * c + 2]
-            inner = ia_ref[18 * t + 6 * c : 18 * t + 6 * c + 6]
-            side = jnp.concatenate([outer[0:1], inner, outer[1:2]], 0)
-            below, above = ordered(even_x, side, sb_ref[spot])
-            planes_ref[c, 0, :, where] = first_ref[spot] + below
-            planes_ref[c, 1, :, where] = last_ref[spot] + above
-        for k in range(2):
-            copies.append(
-                pltpu.make_async_copy(
-                    planes_ref.at[c, k], out_hbm.at[c, 7 * k], sems.at[2 * c + k]
-                )
-            )
-            copies[-1].start()
     for copy in copies:
         copy.wait()
 
@@ -409,8 +368,6 @@
     tiles = length // LANES
     blocks = length // BLOCK
     face = (components * tiles, 8, LANES)
-    inner = (components * tiles * 6, LANES)
-    edge = (components * tiles * 2, LANES)
     tile = (8, LANES)
     flat = (components * tiles, 64, LANES)
     constants = [jnp.asarray(table) for table in tables()]
@@ -430,33 +387,20 @@
     za = exchange(loaded[-2], "gz", 0)
     zb = exchange(loaded[-1], "gz", 1)
     (result,) = call(stiffness_kernel, [flat])(*loaded[:-2])
-    fa, fb, ia, ea, sb = call(
-        face_kernel,
-        [face, face, inner, edge, face],
-        [pltpu.VMEM((2 * components, 64, LANES), F32)],
+    xa, xb, ya, yb = call(
+        face_kernel, [face] * 4, [pltpu.VMEM((2 * components, 64, LANES), F32)]
     )(result, za, zb)
-    fa = mixed_exchange(fa, "gy", 0)
-    fb = mixed_exchange(fb, "gy", 1)
-    ia = mixed_exchange(ia, "gx", 0)
-    (ea,) = call(copy_kernel, [edge])(ea)
-    ea, sb = call(edge_kernel, [edge, face])(ea, sb, fa, fb)
-    sb = mixed_exchange(sb, "gx", 1)
-    ea = mixed_exchange(ea, "gx", 0)
-    vmem = pl.BlockSpec(memory_space=pltpu.VMEM)
-    result, first, last = call(
-        base_kernel,
-        [nodal.shape, face, face],
-        [pltpu.VMEM((components, 6, 8, length), F32), pltpu.SemaphoreType.DMA((3,))],
-        out_specs=[hbm, vmem, vmem],
-    )(result, za, zb, fa, fb)
+    xa = mixed_exchange(xa, "gx", 0)
+    xb = mixed_exchange(xb, "gx", 1)
+    ya, yb = call(edge_kernel, [face, face])(ya, yb, xa, xb)
+    ya = mixed_exchange(ya, "gy", 0)
+    yb = mixed_exchange(yb, "gy", 1)
     (result,) = call(
-        late_kernel,
+        final_kernel,
         [nodal.shape],
-        [pltpu.VMEM((components, 2, 8, length), F32), pltpu.SemaphoreType.DMA((6,))],
-        in_specs=[hbm] + [vmem] * 5,
+        [pltpu.VMEM(nodal.shape, F32), pltpu.SemaphoreType.DMA((components,))],
         out_specs=[hbm],
-        input_output_aliases={0: 0},
-    )(result, first, last, ia, ea, sb)
+    )(result, za, zb, xa, xb, ya, yb)
     return result
 
 

time: 44 us -> 42.4 us (0.964)
  the two profiles are of different devices: /device:TPU:202 before, /device:TPU:232 now
where the time goes in v5:
time: 42.4 us; the launch traced here: 42.1 us
  waiting for transfers between devices  18.4 us (43%)
  starting transfers between devices  16.8 us (40%)
  Pallas kernels  6.82 us (16%)
    ppermute x4, waiting for transfers between devices, mixed_exchange(): return lax.ppermute(array, (axis, 'gz'), found)  18.4 us
    ppermute x4, starting transfers between devices, mixed_exchange(): return lax.ppermute(array, (axis, 'gz'), found)  14.2 us
    pallas_call x1, Pallas kernels, local(): result, = call(stiffness_kernel, [flat])(*loaded[:-2])  3.4 us
    ppermute x2, starting transfers between devices, exchange(): return lax.ppermute(array, axis, pairs_from(start, lax.axis_size(axis)))  2.58 us
    pallas_call x1, Pallas kernels, local(): call(load_kernel, [nodal.shape, (8 * blocks, BLOCK)] + kept + [tile, tile...  1.84 us
    pallas_call x1, Pallas kernels, local(): call(final_kernel, [nodal.shape], [pltpu.VMEM(nodal.shape, F32), pltpu.Se...  1.29 us
  transfers between devices with their start and end apart: 6, of which 3 were waited for; matrix products, arithmetic and copies ran while one was open for 0% of the time, Pallas kernels for 8%

profile of v5, /device:TPU:232, one launch (start us, length us, event | category | flops | bytes accessed | tf_op | source)
XLA Modules:
  0.0 42.1 jit_solution(4052031509024089557)
XLA Ops:
  0.0 1.8 %shard_map.91 = (f32[3,8,8,2048]{3,2,1,0:T(8,128)S(1)}, f32[64,256]{1,0:T(8,128)S(1)}, bf16[128,192]{1,0:T(8,128)(2,1)S(1)}, bf16[128,256]{1,0:T(8,128)(2,1)S(1)...) custom-call(f32[3,8,8,2048]{3,2,1,0:T(8,128)} %u_hbm.1, ...), custom_call_target="tpu_custom_call" | custom-call | flops 1000000 | bytes 1000000 | tf_op jit(solution)/shard_map/pallas_call | solution.py:380
  1.8 1.9 %collective-permute-start = (f32[8,128]{1,0:T(8,128)S(1)}, f32[8,128]{1,0:T(8,128)S(1)}, u32[]{:S(2)}, u32[]{:S(2)}) collective-permute-start(f32[8,128]{1,0:T(8,128)S(1)} %get-tuple-element.27), channel_id=1, source_target_pairs={{0,1},{1,0},{2,3},{3,2},{4,5},{5,4},{6,7},{7,6},{8,9},{9,8},{10,11... | collective-permute-start | bytes 12296 | tf_op jit(solution)/shard_map/ppermute | solution.py:342
  3.8 0.7 %collective-permute-start.1 = (f32[8,128]{1,0:T(8,128)S(1)}, f32[8,128]{1,0:T(8,128)S(1)}, u32[]{:S(2)}, u32[]{:S(2)}) collective-permute-start(f32[8,128]{1,0:T(8,128)S(1)} %get-tuple-element.28), channel_id=1, source_target_pairs={{1,2},{2,1},{3,4},{4,3},{5,6},{6,5},{9,10},{10,9},{11,12},{12,11},... | collective-permute-start | bytes 12296 | tf_op jit(solution)/shard_map/ppermute | solution.py:342
  4.4 3.4 %shard_map.92.local_ref = f32[48,64,128]{2,1,0:T(8,128)S(1)} custom-call(f32[3,8,8,2048]{3,2,1,0:T(8,128)S(1)} %get-tuple-element.20.u_ref, f32[64,256]{1,0:T(8,128)S(1)} %get-tuple-element.21.factor_ref, bf16[128,192]{1,0:T(8,128)(2,1)S(1)} %get-tuple-element.22.gy_ref, bf16[128,256]{1,0:T(8,128)(2,1)S(1)} %get-tuple-element.23.by_ref, ...), custom_call_target="tpu_custom_call" | custom-call | flops 1000000 | bytes 1000000 | tf_op jit(solution)/shard_map/pallas_call | solution.py:389
  7.9 0.0 collective-permute-done.za_ref
  7.9 0.0 collective-permute-done.1.zb_ref
  7.9 0.2 shard_map.93
  8.0 2.7 %collective-permute-start.2 = (f32[48,8,128]{2,1,0:T(8,128)S(1)}, f32[48,8,128]{2,1,0:T(8,128)S(1)}, u32[]{:S(2)}, u32[]{:S(2)}) collective-permute-start(f32[48,8,128]{2,1,0:T(8,128)S(1)} %get-tuple-element.29), channel_id=1, source_target_pairs={{0,128},{128,0},{256,384},{384,256},{129,257},{257,129},{2,130},{1... | collective-permute-start | bytes 589832 | tf_op jit(solution)/shard_map/ppermute | solution.py:351
  10.7 2.7 %collective-permute-start.3 = (f32[48,8,128]{2,1,0:T(8,128)S(1)}, f32[48,8,128]{2,1,0:T(8,128)S(1)}, u32[]{:S(2)}, u32[]{:S(2)}) collective-permute-start(f32[48,8,128]{2,1,0:T(8,128)S(1)} %get-tuple-element.30), channel_id=1, source_target_pairs={{128,256},{256,128},{1,129},{129,1},{257,385},{385,257},{130,258},... | collective-permute-start | bytes 589832 | tf_op jit(solution)/shard_map/ppermute | solution.py:351
  13.4 3.2 %collective-permute-done.2.xa_ref = f32[48,8,128]{2,1,0:T(8,128)S(1)} collective-permute-done((f32[48,8,128]{2,1,0:T(8,128)S(1)}, f32[48,8,128]{2,1,0:T(8,128)S(1)}, u32[]{:S(2)}, u32[]{:S(2)}) %collective-permute-start.2) | collective-permute-done | bytes 196640 | tf_op jit(solution)/shard_map/ppermute | solution.py:351
  16.6 9.3 %collective-permute-done.3.xb_ref = f32[48,8,128]{2,1,0:T(8,128)S(1)} collective-permute-done((f32[48,8,128]{2,1,0:T(8,128)S(1)}, f32[48,8,128]{2,1,0:T(8,128)S(1)}, u32[]{:S(2)}, u32[]{:S(2)}) %collective-permute-start.3) | collective-permute-done | bytes 196640 | tf_op jit(solution)/shard_map/ppermute | solution.py:351
  25.9 0.1 shard_map.94
  26.0 1.9 %collective-permute-start.4 = (f32[48,8,128]{2,1,0:T(8,128)S(1)}, f32[48,8,128]{2,1,0:T(8,128)S(1)}, u32[]{:S(2)}, u32[]{:S(2)}) collective-permute-start(f32[48,8,128]{2,1,0:T(8,128)S(1)} %get-tuple-element.33), channel_id=1, source_target_pairs={{0,8},{8,0},{16,24},{24,16},{32,40},{40,32},{48,56},{56,48},{64,72... | collective-permute-start | bytes 589832 | tf_op jit(solution)/shard_map/ppermute | solution.py:351
  28.0 6.9 %collective-permute-start.5 = (f32[48,8,128]{2,1,0:T(8,128)S(1)}, f32[48,8,128]{2,1,0:T(8,128)S(1)}, u32[]{:S(2)}, u32[]{:S(2)}) collective-permute-start(f32[48,8,128]{2,1,0:T(8,128)S(1)} %get-tuple-element.34), channel_id=1, source_target_pairs={{8,16},{16,8},{24,32},{32,24},{40,48},{48,40},{56,64},{64,56},{72,... | collective-permute-start | bytes 589832 | tf_op jit(solution)/shard_map/ppermute | solution.py:351
  34.9 0.0 collective-permute-done.4.ya_ref
  34.9 5.9 %collective-permute-done.5.yb_ref = f32[48,8,128]{2,1,0:T(8,128)S(1)} collective-permute-done((f32[48,8,128]{2,1,0:T(8,128)S(1)}, f32[48,8,128]{2,1,0:T(8,128)S(1)}, u32[]{:S(2)}, u32[]{:S(2)}) %collective-permute-start.5) | collective-permute-done | bytes 196640 | tf_op jit(solution)/shard_map/ppermute | solution.py:351
  40.8 1.3 %shard_map.95 = f32[3,8,8,2048]{3,2,1,0:T(8,128)} custom-call(f32[48,64,128]{2,1,0:T(8,128)S(1)} %shard_map.92.local_ref, f32[8,128]{1,0:T(8,128)S(1)} %collective-permute-done.za_ref, f32[8,128]{1,0:T(8,128)S(1)} %collective-permute-done.1.zb_ref, f32[48,8,128]{2,1,0:T(8,128)S(1)} %collective-permute-done.2.xa_ref, ...), custom_call_target="tpu_custom_call" | custom-call | flops 1000000 | bytes 1000000 | tf_op jit(solution)/shard_map/pallas_call | solution.py:398
Async XLA Ops:
  1.8 6.0 %collective-permute-start = (f32[8,128]{1,0:T(8,128)S(1)}, f32[8,128]{1,0:T(8,128)S(1)}, u32[]{:S(2)}, u32[]{:S(2)}) collective-permute-start(f32[8,128]{1,0:T(8,128)S(1)} %get-tuple-element.27), channel_id=1, source_target_pairs={{0,1},{1,0},{2,3},{3,2},{4,5},{5,4},{6,7},{7,6},{8,9},{9,8},{10,11... | collective-permute-start | bytes 12296 | tf_op jit(solution)/shard_map/ppermute | solution.py:342
  3.8 4.1 %collective-permute-start.1 = (f32[8,128]{1,0:T(8,128)S(1)}, f32[8,128]{1,0:T(8,128)S(1)}, u32[]{:S(2)}, u32[]{:S(2)}) collective-permute-start(f32[8,128]{1,0:T(8,128)S(1)} %get-tuple-element.28), channel_id=1, source_target_pairs={{1,2},{2,1},{3,4},{4,3},{5,6},{6,5},{9,10},{10,9},{11,12},{12,11},... | collective-permute-start | bytes 12296 | tf_op jit(solution)/shard_map/ppermute | solution.py:342
  8.0 8.6 %collective-permute-start.2 = (f32[48,8,128]{2,1,0:T(8,128)S(1)}, f32[48,8,128]{2,1,0:T(8,128)S(1)}, u32[]{:S(2)}, u32[]{:S(2)}) collective-permute-start(f32[48,8,128]{2,1,0:T(8,128)S(1)} %get-tuple-element.29), channel_id=1, source_target_pairs={{0,128},{128,0},{256,384},{384,256},{129,257},{257,129},{2,130},{1... | collective-permute-start | bytes 589832 | tf_op jit(solution)/shard_map/ppermute | solution.py:351
  10.7 15.2 %collective-permute-start.3 = (f32[48,8,128]{2,1,0:T(8,128)S(1)}, f32[48,8,128]{2,1,0:T(8,128)S(1)}, u32[]{:S(2)}, u32[]{:S(2)}) collective-permute-start(f32[48,8,128]{2,1,0:T(8,128)S(1)} %get-tuple-element.30), channel_id=1, source_target_pairs={{128,256},{256,128},{1,129},{129,1},{257,385},{385,257},{130,258},... | collective-permute-start | bytes 589832 | tf_op jit(solution)/shard_map/ppermute | solution.py:351
  26.0 8.9 %collective-permute-start.4 = (f32[48,8,128]{2,1,0:T(8,128)S(1)}, f32[48,8,128]{2,1,0:T(8,128)S(1)}, u32[]{:S(2)}, u32[]{:S(2)}) collective-permute-start(f32[48,8,128]{2,1,0:T(8,128)S(1)} %get-tuple-element.33), channel_id=1, source_target_pairs={{0,8},{8,0},{16,24},{24,16},{32,40},{40,32},{48,56},{56,48},{64,72... | collective-permute-start | bytes 589832 | tf_op jit(solution)/shard_map/ppermute | solution.py:351
  28.0 12.9 %collective-permute-start.5 = (f32[48,8,128]{2,1,0:T(8,128)S(1)}, f32[48,8,128]{2,1,0:T(8,128)S(1)}, u32[]{:S(2)}, u32[]{:S(2)}) collective-permute-start(f32[48,8,128]{2,1,0:T(8,128)S(1)} %get-tuple-element.34), channel_id=1, source_target_pairs={{8,16},{16,8},{24,32},{32,24},{40,48},{48,40},{56,64},{64,56},{72,... | collective-permute-start | bytes 589832 | tf_op jit(solution)/shard_map/ppermute | solution.py:351
